TPU v7x, 256 devices: a 2x2x32 block of a 4x8x32 slice. The times are simulated.
256 devices in a mesh: member: 4 (over x, y), block: 64 (over z, core).
Axes of the slice: x: 2, y: 2, z: 32, core: 2. Of those that a mesh axis runs over, the one named last changes fastest.
The devices are a block of a 4x8x32 slice.
Arguments:
- grid_in: bfloat16 [262144, 128], P(('member', 'block')), parts along dimension 0, may hold values from -6 to 6
- dest_block: int32 [262144, 1], P(('member', 'block')), parts along dimension 0, may hold values from 0 to 63, as said below
- dest_node: int32 [262144], P(('member', 'block')), parts along dimension 0, may hold values from 0 to 255
- neighbour_mask: int32 [65536, 4], P(('member', 'block')), parts along dimension 0, may hold values 0 or 1
- mesh_embed: bfloat16 [65536, 512], P(('member', 'block')), parts along dimension 0, may hold values from -6 to 6
- w_in: bfloat16 [128, 512], replicated, may hold values from -0.5 to 0.5
- in_bias: bfloat16 [512], replicated, may hold values from -3 to 3
- w_grid: bfloat16 [512, 512], replicated, may hold values from -0.25 to 0.25
- w_enc: bfloat16 [512, 512], replicated, may hold values from -0.25 to 0.25
- attn_gain: bfloat16 [2, 512], replicated, may hold values from 0.099609375 to 1.8984375
- w_query: bfloat16 [2, 512, 512], replicated, may hold values from -0.25 to 0.25
- w_key: bfloat16 [2, 512, 512], replicated, may hold values from -0.25 to 0.25
- w_value: bfloat16 [2, 512, 512], replicated, may hold values from -0.25 to 0.25
- w_out: bfloat16 [2, 512, 512], replicated, may hold values from -0.25 to 0.25
- mlp_gain: bfloat16 [2, 512], replicated, may hold values from 0.099609375 to 1.8984375
- w_up: bfloat16 [2, 512, 512], replicated, may hold values from -0.25 to 0.25
- w_down: bfloat16 [2, 512, 512], replicated, may hold values from -0.25 to 0.25
- dec_gain: bfloat16 [512], replicated, may hold values from 0.099609375 to 1.8984375
- w_dec: bfloat16 [512, 512], replicated, may hold values from -0.25 to 0.25
- w_head: bfloat16 [512, 512], replicated, may hold values from -0.25 to 0.25
- w_final: bfloat16 [512, 128], replicated, may hold values from -0.25 to 0.25
Outputs:
- grid_out: bfloat16 [262144, 128], P(('member', 'block')), parts along dimension 0
There are 4 independent parts, one for each index of `member`. A program takes and returns all parts, laid end to end along the dimension named above; an argument that names none is the same for every part. Nothing has to cross between parts.
Inputs may be any that keep to these rules, and one draw needn't show every extreme that they name: `dest_block`: A grid point of block b maps into one of the mesh blocks b-2, b-1, b, b+1, b+2 (modulo 64); within the 1024 rows of one block exactly 512 name one of these five, and the others name fewer.
All inputs are finite; a program needn't handle non-finite values. No bound on the sum of `neighbour_mask` on one device may be relied on, other than what follows from the above.
Results may differ from a plain program's by a relative error of at most 0.014.
Values may be sent and summed in bfloat16 or wider, within the bound.
A program may use at most 64 MiB of HBM per device.

v0:
```python
import jax
import jax.numpy as jnp
from jax import lax
from jax.sharding import PartitionSpec as P

HEADS = 8
LAYERS = 2


def shifted(value, axis, steps):
    count = lax.axis_size(axis)
    pairs = [(source, (source + steps) % count) for source in range(count)]
    return lax.ppermute(value, axis, pairs)


def rms_norm(values, gain):
    return (
        values
        * lax.rsqrt(jnp.mean(values * values, axis=-1, keepdims=True) + 1e-06)
        * gain.astype(jnp.float32)
    )


def grid_mlp(rows, w_in, in_bias, w_grid):
    grid_hidden = jax.nn.silu(
        jnp.dot(rows, w_in, preferred_element_type=jnp.float32) + in_bias.astype(jnp.float32)
    ).astype(jnp.bfloat16)
    return jnp.dot(grid_hidden, w_grid, preferred_element_type=jnp.float32).astype(jnp.bfloat16)


def attend(query_rows, key_rows, value_rows, allowed):
    row_count, feature_width = query_rows.shape
    head_dim = feature_width // HEADS
    queries = query_rows.reshape(row_count, HEADS, head_dim).transpose(1, 0, 2)
    keys_near = key_rows.reshape(-1, HEADS, head_dim).transpose(1, 0, 2)
    values_near = value_rows.reshape(-1, HEADS, head_dim).transpose(1, 0, 2)

    def single(operands):
        query_head, key_head, value_head = operands
        scores = lax.dot_general(
            query_head, key_head, (((1,), (1,)), ((), ())), preferred_element_type=jnp.float32
        ) * head_dim ** (-0.5)
        scores = jnp.where(allowed[:, :, None], scores.reshape(row_count, 5, -1), -jnp.inf).reshape(
            row_count, -1
        )
        largest = jnp.max(scores, axis=-1, keepdims=True)
        exponent = jnp.exp(scores - largest)
        softmax_weights = (exponent / jnp.sum(exponent, axis=-1, keepdims=True)).astype(
            jnp.bfloat16
        )
        return jnp.dot(softmax_weights, value_head, preferred_element_type=jnp.float32).astype(
            jnp.bfloat16
        )

    attended = lax.map(single, (queries, keys_near, values_near))
    return attended.transpose(1, 0, 2).reshape(row_count, feature_width)


def nearby_states(normed):
    pieces = []
    for offset in (-2, -1, 0, 1, 2):
        if offset == 0:
            pieces.append(normed)
        else:
            pieces.append(shifted(normed, "block", -offset))
    return jnp.concatenate(pieces, axis=0)


def body(
    grid_in,
    dest_block,
    dest_node,
    neighbour_mask,
    mesh_embed,
    w_in,
    in_bias,
    w_grid,
    w_enc,
    attn_gain,
    w_query,
    w_key,
    w_value,
    w_out,
    mlp_gain,
    w_up,
    w_down,
    dec_gain,
    w_dec,
    w_head,
    w_final,
):
    block_count = lax.axis_size("block")
    my_index = lax.axis_index("block")
    grid_rows = grid_in.shape[0]
    mesh_rows = mesh_embed.shape[0]
    feature_width = w_enc.shape[0]
    capacity = grid_rows // 2
    grid_feat = grid_mlp(grid_in, w_in, in_bias, w_grid)
    destination = dest_block[:, 0]
    relative = (destination - my_index) % block_count
    offset_index = jnp.where(relative > block_count // 2, relative - block_count, relative) + 2
    one_hot = (offset_index[:, None] == jnp.arange(5, dtype=jnp.int32)[None, :]).astype(jnp.int32)
    earlier = jnp.cumsum(one_hot, axis=0) - one_hot
    slot_index = jnp.sum(earlier * one_hot, axis=1)
    placement_index = offset_index * capacity + slot_index
    source_row = (
        jnp.full((5 * capacity,), grid_rows, jnp.int32)
        .at[placement_index]
        .set(jnp.arange(grid_rows, dtype=jnp.int32))
    )
    node_slots = (
        jnp.full((5 * capacity,), -1, jnp.int32)
        .at[placement_index]
        .set(dest_node)
        .reshape(5, capacity)
    )
    padded = jnp.concatenate([grid_in, jnp.zeros((1, grid_in.shape[1]), jnp.bfloat16)], axis=0)
    outgoing = padded[source_row].reshape(5, capacity, grid_in.shape[1])
    received = [None] * 5
    received_nodes = [None] * 5
    received[2] = outgoing[2]
    received_nodes[2] = node_slots[2]
    for offset in (-2, -1, 1, 2):
        got_rows, got_nodes = shifted(
            (outgoing[offset + 2], node_slots[offset + 2]), "block", offset
        )
        received[offset + 2] = got_rows
        received_nodes[offset + 2] = got_nodes
    incoming = jnp.stack(received).reshape(5 * capacity, grid_in.shape[1])
    arrived = jnp.stack(received_nodes)
    incoming = grid_mlp(incoming, w_in, in_bias, w_grid)
    matches = arrived.reshape(-1)[:, None] == jnp.arange(mesh_rows, dtype=jnp.int32)[None, :]
    summed = lax.dot_general(
        matches.astype(jnp.bfloat16),
        incoming,
        (((0,), (0,)), ((), ())),
        preferred_element_type=jnp.float32,
    )
    counts = jnp.sum(matches.astype(jnp.float32), axis=0)
    mean_rows = (summed / jnp.maximum(counts, 1.0)[:, None]).astype(jnp.bfloat16)
    mesh_state = mesh_embed.astype(jnp.float32) + jnp.dot(
        mean_rows, w_enc, preferred_element_type=jnp.float32
    )
    allowed = (
        jnp.concatenate(
            [neighbour_mask[:, :2], jnp.ones((mesh_rows, 1), jnp.int32), neighbour_mask[:, 2:]],
            axis=1,
        )
        > 0
    )
    for layer_index in range(LAYERS):
        normed = rms_norm(mesh_state, attn_gain[layer_index]).astype(jnp.bfloat16)
        query_rows = jnp.dot(
            normed, w_query[layer_index], preferred_element_type=jnp.float32
        ).astype(jnp.bfloat16)
        nearby = nearby_states(normed)
        keys_near = jnp.dot(nearby, w_key[layer_index], preferred_element_type=jnp.float32).astype(
            jnp.bfloat16
        )
        values_near = jnp.dot(
            nearby, w_value[layer_index], preferred_element_type=jnp.float32
        ).astype(jnp.bfloat16)
        attended = attend(query_rows, keys_near, values_near, allowed)
        mesh_state = mesh_state + jnp.dot(
            attended, w_out[layer_index], preferred_element_type=jnp.float32
        )
        normed_second = rms_norm(mesh_state, mlp_gain[layer_index]).astype(jnp.bfloat16)
        up_hidden = jax.nn.silu(
            jnp.dot(normed_second, w_up[layer_index], preferred_element_type=jnp.float32)
        ).astype(jnp.bfloat16)
        mesh_state = mesh_state + jnp.dot(
            up_hidden, w_down[layer_index], preferred_element_type=jnp.float32
        )
    decoded = rms_norm(mesh_state, dec_gain).astype(jnp.bfloat16)
    answer_rows = decoded[jnp.clip(arrived, 0, mesh_rows - 1)]
    returned = [None] * 5
    returned[2] = answer_rows[2]
    for offset in (-2, -1, 1, 2):
        returned[offset + 2] = shifted(answer_rows[offset + 2], "block", -offset)
    gathered = jnp.stack(returned).reshape(-1, feature_width)[placement_index]
    grid_mix = (
        grid_feat.astype(jnp.float32) + jnp.dot(gathered, w_dec, preferred_element_type=jnp.float32)
    ).astype(jnp.bfloat16)
    head_rows = jax.nn.silu(jnp.dot(grid_mix, w_head, preferred_element_type=jnp.float32)).astype(
        jnp.bfloat16
    )
    return jnp.dot(head_rows, w_final, preferred_element_type=jnp.float32).astype(jnp.bfloat16)


def solution(mesh):
    placed = (
        P(("member", "block"), None),
        P(("member", "block"), None),
        P(("member", "block")),
        P(("member", "block"), None),
        P(("member", "block"), None),
        P(),
        P(),
        P(),
        P(),
        P(),
        P(),
        P(),
        P(),
        P(),
        P(),
        P(),
        P(),
        P(),
        P(),
        P(),
        P(),
    )
    return jax.shard_map(
        body, mesh=mesh, in_specs=placed, out_specs=P(("member", "block"), None), check_vma=False
    )
```

profile of v0, /device:TPU:46, one launch (start us, length us, event | category | flops | bytes accessed | tf_op | source)
XLA Modules:
  0.0 222.0 jit_solution(13649093172846690494)
XLA Ops:
  3.5 4.5 %scatter_custom_fusion = s32[2560]{0:T(1024)S(1)} fusion(s32[1024]{0:T(1024)S(1)} %bitcast.244, s32[1024]{0:T(1024)} %param.27, s32[]{:T(128)} %constant.63.clone.1), kind=kCustom, calls=%fused_computation.158 | custom fusion | bytes 10752 | tf_op jit(solution)/shard_map/scatter | solution.py:114
  8.0 23.1 %collective-permute-start = (s32[512]{0:T(512)S(1)}, s32[512]{0:T(512)S(1)}, u32[]{:S(2)}, u32[]{:S(2)}) collective-permute-start(s32[512]{0:T(512)S(1)} %get-tuple-element.135), channel_id=1, source_target_pairs={{0,62},{1,63},{2,0},{3,1},{4,2},{5,3},{6,4},{7,5},{8,6},{9,7},{10,... | collective-permute-start | bytes 6152 | tf_op jit(solution)/shard_map/ppermute | solution.py:13
  32.4 4.3 %scatter_custom_fusion.1 = s32[2560]{0:T(1024)S(1)} fusion(s32[1024]{0:T(1024)S(1)} %bitcast.245, s32[1024]{0:T(1024)S(1)} %iota.15, s32[]{:T(128)} %constant.100.clone.1), kind=kCustom, calls=%fused_computation.156 | custom fusion | bytes 10244 | tf_op jit(solution)/shard_map/scatter | solution.py:109
  40.9 5.1 %gather_fusion = bf16[2560,128]{1,0:T(8,128)(2,1)S(1)} fusion(bf16[1025,128]{1,0:T(8,128)(2,1)S(1)} %concatenate.19, s32[3072]{0:T(1024)S(1)} %get-tuple-element.153), kind=kCustom, calls=%fused_computation | custom fusion | bytes 1320960 | tf_op jit(solution)/shard_map/gather | solution.py:118
  46.0 2.6 %collective-permute-start.4 = (bf16[512,128]{1,0:T(8,128)(2,1)S(1)}, bf16[512,128]{1,0:T(8,128)(2,1)S(1)}, u32[]{:S(2)}, u32[]{:S(2)}) collective-permute-start(bf16[512,128]{1,0:T(8,128)(2,1)S(1)} %get-tuple-element.130), channel_id=1, source_target_pairs={{0,62},{1,63},{2,0},{3,1},{4,2},{5,3},{6,4},{7,5},{8,6},{9,7},{10,... | collective-permute-start | bytes 393224 | tf_op jit(solution)/shard_map/ppermute | solution.py:13
  53.6 2.2 collective-permute-done.6
  57.0 3.8 %convolution_convert_fusion.2 = bf16[2560,512]{1,0:T(8,128)(2,1)} fusion(bf16[512,512]{1,0:T(8,128)(2,1)S(1)} %copy-done, bf16[2560,128]{1,0:T(8,128)(2,1)S(1)} %bitcast.236, bf16[128,512]{1,0:T(8,128)(2,1)S(1)} %copy-done.14, f32[512]{0:T(512)S(1)} %convert_element_type.107), kind=kOutput, calls=%fused_computation.38 | convolution fusion | flops 1686896640 | bytes 3934208 | tf_op jit(solution)/shard_map/dot_general | solution.py:28
  60.9 3.4 %multiply_reduce_fusion.4 = (f32[256]{0:T(256)S(1)}, f32[256,512]{1,0:T(8,128)S(1)}) fusion(bf16[512,512]{1,0:T(8,128)(2,1)S(1)} %copy-done.12, bf16[2560,512]{1,0:T(8,128)(2,1)} %convolution_convert_fusion.2, s32[2560]{0:T(1024)S(1)} %eq.50, f32[256]{0:T(256)S(1)} %broadcast_maximum_fusion, bf16[256,512]{1,0:T(8,128)(2,1)S(1)} %copy-done.13), kind=kOutput, calls=%fused_computation.107 | convolution fusion | flops 806747904 | bytes 3944448 | tf_op jit(solution)/shard_map/dot_general | solution.py:141
  65.3 2.6 %collective-permute-start.10 = (bf16[256,512]{1,0:T(8,128)(2,1)S(1)}, bf16[256,512]{1,0:T(8,128)(2,1)S(1)}, u32[]{:S(2)}, u32[]{:S(2)}) collective-permute-start(bf16[256,512]{1,0:T(8,128)(2,1)S(1)} %multiply_convert_fusion.13), channel_id=1, source_target_pairs={{0,63},{1,0},{2,1},{3,2},{4,3},{5,4},{6,5},{7,6},{8,7},{9,8},{10,9... | collective-permute-start | bytes 786440 | tf_op jit(solution)/shard_map/ppermute | solution.py:13
  71.8 3.1 %collective-permute-done.8 = bf16[256,512]{1,0:T(8,128)(2,1)S(1)} collective-permute-done((bf16[256,512]{1,0:T(8,128)(2,1)S(1)}, bf16[256,512]{1,0:T(8,128)(2,1)S(1)}, u32[]{:S(2)}, u32[]{:S(2)}) %collective-permute-start.8) | collective-permute-done | bytes 262176 | tf_op jit(solution)/shard_map/ppermute | solution.py:13
  75.0 2.5 %collective-permute-done.9 = bf16[256,512]{1,0:T(8,128)(2,1)S(1)} collective-permute-done((bf16[256,512]{1,0:T(8,128)(2,1)S(1)}, bf16[256,512]{1,0:T(8,128)(2,1)S(1)}, u32[]{:S(2)}, u32[]{:S(2)}) %collective-permute-start.9) | collective-permute-done | bytes 262176 | tf_op jit(solution)/shard_map/ppermute | solution.py:13
  77.7 2.0 convolution_convert_fusion.6
  79.7 3.2 %copy.43 = bf16[1280,8,64]{2,0,1:T(8,128)(2,1)S(1)} copy(bf16[1280,8,64]{0,2,1:T(8,128)(2,1)} %bitcast.229) | data formatting | bytes 2621440 | tf_op jit(solution)/shard_map/reshape | solution.py:35
  82.9 3.4 %convolution_convert_fusion.5 = bf16[1280,512]{0,1:T(8,128)(2,1)} fusion(bf16[1280,512]{1,0:T(8,128)(2,1)} %copy-done.6, bf16[2,512,512]{2,1,0:T(8,128)(2,1)} %param.37), kind=kOutput, calls=%fused_computation.41 | convolution fusion | flops 671744000 | bytes 3145728 | tf_op jit(solution)/shard_map/dot_general | solution.py:160
  86.3 3.7 %copy.44 = bf16[1280,8,64]{2,0,1:T(8,128)(2,1)} copy(bf16[1280,8,64]{0,2,1:T(8,128)(2,1)} %bitcast.228) | data formatting | bytes 2621440 | tf_op jit(solution)/shard_map/reshape | solution.py:36
  90.1 28.6 %while.20 = (s32[]{:T(128)}, bf16[8,256,64]{1,2,0:T(8,128)(2,1)S(1)}, pred[256,5]{0,1:T(8,128)(4,1)S(1)}, bf16[8,256,64]{1,2,0:T(8,128)(2,1)}, bf16[8,1280,64]{2...) while((s32[]{:T(128)}, bf16[8,256,64]{1,2,0:T(8,128)(2,1)S(1)}, ...), condition=%wide.region_10.11_spmd, body=%wide.region_7.10_spmd.sunk | while | flops 86523392 | bytes 5972301 | solution.py:55
  122.6 2.9 %collective-permute-start.14 = (bf16[256,512]{1,0:T(8,128)(2,1)S(1)}, bf16[256,512]{1,0:T(8,128)(2,1)S(1)}, u32[]{:S(2)}, u32[]{:S(2)}) collective-permute-start(bf16[256,512]{1,0:T(8,128)(2,1)S(1)} %multiply_convert_fusion.8), channel_id=1, source_target_pairs={{0,63},{1,0},{2,1},{3,2},{4,3},{5,4},{6,5},{7,6},{8,7},{9,8},{10,9... | collective-permute-start | bytes 786440 | tf_op jit(solution)/shard_map/ppermute | solution.py:13
  125.5 2.1 collective-permute-start.15
  129.8 2.9 %collective-permute-done.12 = bf16[256,512]{1,0:T(8,128)(2,1)S(1)} collective-permute-done((bf16[256,512]{1,0:T(8,128)(2,1)S(1)}, bf16[256,512]{1,0:T(8,128)(2,1)S(1)}, u32[]{:S(2)}, u32[]{:S(2)}) %collective-permute-start.12) | collective-permute-done | bytes 262176 | tf_op jit(solution)/shard_map/ppermute | solution.py:13
  132.9 2.1 collective-permute-done.15
  137.1 2.0 convolution_convert_fusion.3
  139.0 3.2 %copy.47 = bf16[1280,8,64]{2,0,1:T(8,128)(2,1)S(1)} copy(bf16[1280,8,64]{0,2,1:T(8,128)(2,1)} %bitcast.227) | data formatting | bytes 2621440 | tf_op jit(solution)/shard_map/reshape | solution.py:35
  142.3 3.8 %copy.48 = bf16[1280,8,64]{2,0,1:T(8,128)(2,1)} copy(bf16[1280,8,64]{0,2,1:T(8,128)(2,1)} %bitcast.226) | data formatting | bytes 2621440 | tf_op jit(solution)/shard_map/reshape | solution.py:36
  146.0 28.6 %while.21 = (s32[]{:T(128)}, bf16[8,256,64]{1,2,0:T(8,128)(2,1)S(1)}, pred[256,5]{0,1:T(8,128)(4,1)S(1)}, bf16[8,256,64]{1,2,0:T(8,128)(2,1)}, bf16[8,1280,64]{2...) while((s32[]{:T(128)}, bf16[8,256,64]{1,2,0:T(8,128)(2,1)S(1)}, ...), condition=%wide.region_16.17_spmd, body=%wide.region_13.16_spmd.sunk | while | flops 86523392 | bytes 5972301 | solution.py:55
  178.3 7.7 %gather_fusion.1 = bf16[2560,512]{1,0:T(8,128)(2,1)S(1)} fusion(bf16[256,512]{1,0:T(8,128)(2,1)S(1)} %multiply_convert_fusion.3, s32[3072]{0:T(1024)S(1)} %get-tuple-element.152), kind=kCustom, calls=%fused_computation.1 | custom fusion | bytes 5253120 | tf_op jit(solution)/shard_map/gather | solution.py:175
  188.1 3.1 %convolution_convert_fusion.7 = bf16[1024,512]{1,0:T(8,128)(2,1)} fusion(bf16[512,512]{1,0:T(8,128)(2,1)S(1)} %copy-done, bf16[1024,128]{1,0:T(8,128)(2,1)S(1)} %copy-done.4, bf16[128,512]{1,0:T(8,128)(2,1)} %param.30, f32[512]{0:T(512)S(1)} %convert_element_type.107), kind=kOutput, calls=%fused_computation.49 | convolution fusion | flops 674758656 | bytes 1968128 | tf_op jit(solution)/shard_map/dot_general | solution.py:28
  191.2 2.9 %collective-permute-start.18 = (bf16[512,512]{1,0:T(8,128)(2,1)}, bf16[512,512]{1,0:T(8,128)(2,1)S(1)}, u32[]{:S(2)}, u32[]{:S(2)}) collective-permute-start(bf16[512,512]{1,0:T(8,128)(2,1)} %get-tuple-element.124), channel_id=1, source_target_pairs={{0,63},{1,0},{2,1},{3,2},{4,3},{5,4},{6,5},{7,6},{8,7},{9,8},{10,9... | collective-permute-start | bytes 1572872 | tf_op jit(solution)/shard_map/ppermute | solution.py:13
  194.1 2.5 %collective-permute-start.19 = (bf16[512,512]{1,0:T(8,128)(2,1)}, bf16[512,512]{1,0:T(8,128)(2,1)S(1)}, u32[]{:S(2)}, u32[]{:S(2)}) collective-permute-start(bf16[512,512]{1,0:T(8,128)(2,1)} %get-tuple-element.123), channel_id=1, source_target_pairs={{0,62},{1,63},{2,0},{3,1},{4,2},{5,3},{6,4},{7,5},{8,6},{9,7},{10,... | collective-permute-start | bytes 1572872 | tf_op jit(solution)/shard_map/ppermute | solution.py:13
  196.6 8.3 %collective-permute-done.16 = bf16[512,512]{1,0:T(8,128)(2,1)} collective-permute-done((bf16[512,512]{1,0:T(8,128)(2,1)}, bf16[512,512]{1,0:T(8,128)(2,1)}, u32[]{:S(2)}, u32[]{:S(2)}) %collective-permute-start.16) | collective-permute-done | bytes 524320 | tf_op jit(solution)/shard_map/ppermute | solution.py:13
  209.1 3.3 %collective-permute-done.19 = bf16[512,512]{1,0:T(8,128)(2,1)S(1)} collective-permute-done((bf16[512,512]{1,0:T(8,128)(2,1)}, bf16[512,512]{1,0:T(8,128)(2,1)S(1)}, u32[]{:S(2)}, u32[]{:S(2)}) %collective-permute-start.19) | collective-permute-done | bytes 524320 | tf_op jit(solution)/shard_map/ppermute | solution.py:13
  212.4 5.1 %gather_fusion.2 = bf16[1024,512]{1,0:T(8,128)(2,1)} fusion(bf16[2560,512]{1,0:T(8,128)(2,1)S(1)} %bitcast.221, s32[1024]{0:T(1024)S(1)} %broadcast_clamp_fusion), kind=kCustom, calls=%fused_computation.2 | custom fusion | bytes 2101248 | tf_op jit(solution)/shard_map/gather | solution.py:180
  217.5 3.4 %multiply_convert_fusion.1 = bf16[1024,512]{1,0:T(8,128)(2,1)S(1)} fusion(bf16[512,512]{1,0:T(8,128)(2,1)} %param.44, bf16[1024,512]{1,0:T(8,128)(2,1)} %convolution_convert_fusion.7, bf16[1024,512]{1,0:T(8,128)(2,1)} %gather_fusion.2, bf16[512,512]{1,0:T(8,128)(2,1)} %param.43), kind=kOutput, calls=%fused_computation.46 | convolution fusion | flops 1077936128 | bytes 4194304 | tf_op jit(solution)/shard_map/dot_general | solution.py:184
  (210 shorter events, 96.0 us)
Async XLA Ops:
  0.0 57.0 %copy-start = (bf16[512,512]{1,0:T(8,128)(2,1)S(1)}, bf16[512,512]{1,0:T(8,128)(2,1)}, u32[]{:S(2)}) copy-start(bf16[512,512]{1,0:T(8,128)(2,1)} %param.32) | copy-start | bytes 1572868
  8.0 32.8 %collective-permute-start = (s32[512]{0:T(512)S(1)}, s32[512]{0:T(512)S(1)}, u32[]{:S(2)}, u32[]{:S(2)}) collective-permute-start(s32[512]{0:T(512)S(1)} %get-tuple-element.135), channel_id=1, source_target_pairs={{0,62},{1,63},{2,0},{3,1},{4,2},{5,3},{6,4},{7,5},{8,6},{9,7},{10,... | collective-permute-start | bytes 6152 | tf_op jit(solution)/shard_map/ppermute | solution.py:13
  31.1 9.6 %collective-permute-start.1 = (s32[512]{0:T(512)S(1)}, s32[512]{0:T(512)S(1)}, u32[]{:S(2)}, u32[]{:S(2)}) collective-permute-start(s32[512]{0:T(512)S(1)} %get-tuple-element.134), channel_id=1, source_target_pairs={{0,63},{1,0},{2,1},{3,2},{4,3},{5,4},{6,5},{7,6},{8,7},{9,8},{10,9... | collective-permute-start | bytes 6152 | tf_op jit(solution)/shard_map/ppermute | solution.py:13
  31.1 9.6 %collective-permute-start.2 = (s32[512]{0:T(512)S(1)}, s32[512]{0:T(512)S(1)}, u32[]{:S(2)}, u32[]{:S(2)}) collective-permute-start(s32[512]{0:T(512)S(1)} %get-tuple-element.132), channel_id=1, source_target_pairs={{0,1},{1,2},{2,3},{3,4},{4,5},{5,6},{6,7},{7,8},{8,9},{9,10},{10,1... | collective-permute-start | bytes 6152 | tf_op jit(solution)/shard_map/ppermute | solution.py:13
  31.6 9.2 %collective-permute-start.3 = (s32[512]{0:T(512)S(1)}, s32[512]{0:T(512)S(1)}, u32[]{:S(2)}, u32[]{:S(2)}) collective-permute-start(s32[512]{0:T(512)S(1)} %get-tuple-element.131), channel_id=1, source_target_pairs={{0,2},{1,3},{2,4},{3,5},{4,6},{5,7},{6,8},{7,9},{8,10},{9,11},{10,... | collective-permute-start | bytes 6152 | tf_op jit(solution)/shard_map/ppermute | solution.py:13
  46.0 11.0 %copy-start.14 = (bf16[128,512]{1,0:T(8,128)(2,1)S(1)}, bf16[128,512]{1,0:T(8,128)(2,1)}, u32[]{:S(2)}) copy-start(bf16[128,512]{1,0:T(8,128)(2,1)} %param.30) | copy-start | bytes 393220
  46.0 6.1 %collective-permute-start.4 = (bf16[512,128]{1,0:T(8,128)(2,1)S(1)}, bf16[512,128]{1,0:T(8,128)(2,1)S(1)}, u32[]{:S(2)}, u32[]{:S(2)}) collective-permute-start(bf16[512,128]{1,0:T(8,128)(2,1)S(1)} %get-tuple-element.130), channel_id=1, source_target_pairs={{0,62},{1,63},{2,0},{3,1},{4,2},{5,3},{6,4},{7,5},{8,6},{9,7},{10,... | collective-permute-start | bytes 393224 | tf_op jit(solution)/shard_map/ppermute | solution.py:13
  48.6 4.9 %collective-permute-start.5 = (bf16[512,128]{1,0:T(8,128)(2,1)S(1)}, bf16[512,128]{1,0:T(8,128)(2,1)S(1)}, u32[]{:S(2)}, u32[]{:S(2)}) collective-permute-start(bf16[512,128]{1,0:T(8,128)(2,1)S(1)} %get-tuple-element.129), channel_id=1, source_target_pairs={{0,63},{1,0},{2,1},{3,2},{4,3},{5,4},{6,5},{7,6},{8,7},{9,8},{10,9... | collective-permute-start | bytes 393224 | tf_op jit(solution)/shard_map/ppermute | solution.py:13
  49.4 6.4 %collective-permute-start.6 = (bf16[512,128]{1,0:T(8,128)(2,1)S(1)}, bf16[512,128]{1,0:T(8,128)(2,1)S(1)}, u32[]{:S(2)}, u32[]{:S(2)}) collective-permute-start(bf16[512,128]{1,0:T(8,128)(2,1)S(1)} %get-tuple-element.128), channel_id=1, source_target_pairs={{0,1},{1,2},{2,3},{3,4},{4,5},{5,6},{6,7},{7,8},{8,9},{9,10},{10,1... | collective-permute-start | bytes 393224 | tf_op jit(solution)/shard_map/ppermute | solution.py:13
  49.4 7.6 %collective-permute-start.7 = (bf16[512,128]{1,0:T(8,128)(2,1)S(1)}, bf16[512,128]{1,0:T(8,128)(2,1)S(1)}, u32[]{:S(2)}, u32[]{:S(2)}) collective-permute-start(bf16[512,128]{1,0:T(8,128)(2,1)S(1)} %get-tuple-element.127), channel_id=1, source_target_pairs={{0,2},{1,3},{2,4},{3,5},{4,6},{5,7},{6,8},{7,9},{8,10},{9,11},{10,... | collective-permute-start | bytes 393224 | tf_op jit(solution)/shard_map/ppermute | solution.py:13
  57.0 3.9 %copy-start.12 = (bf16[512,512]{1,0:T(8,128)(2,1)S(1)}, bf16[512,512]{1,0:T(8,128)(2,1)}, u32[]{:S(2)}) copy-start(bf16[512,512]{1,0:T(8,128)(2,1)} %param.33) | copy-start | bytes 1572868
  57.0 3.9 %copy-start.13 = (bf16[256,512]{1,0:T(8,128)(2,1)S(1)}, bf16[256,512]{1,0:T(8,128)(2,1)}, u32[]{:S(2)}) copy-start(bf16[256,512]{1,0:T(8,128)(2,1)} %param.29) | copy-start | bytes 786436
  64.3 13.2 %copy-start.2 = (f32[256,512]{1,0:T(8,128)}, f32[256,512]{1,0:T(8,128)S(1)}, u32[]{:S(2)}) copy-start(f32[256,512]{1,0:T(8,128)S(1)} %get-tuple-element.143) | copy-start | bytes 1572868
  64.4 10.5 %collective-permute-start.8 = (bf16[256,512]{1,0:T(8,128)(2,1)S(1)}, bf16[256,512]{1,0:T(8,128)(2,1)S(1)}, u32[]{:S(2)}, u32[]{:S(2)}) collective-permute-start(bf16[256,512]{1,0:T(8,128)(2,1)S(1)} %multiply_convert_fusion.13), channel_id=1, source_target_pairs={{0,2},{1,3},{2,4},{3,5},{4,6},{5,7},{6,8},{7,9},{8,10},{9,11},{10,... | collective-permute-start | bytes 786440 | tf_op jit(solution)/shard_map/ppermute | solution.py:13
  64.7 12.8 %collective-permute-start.9 = (bf16[256,512]{1,0:T(8,128)(2,1)S(1)}, bf16[256,512]{1,0:T(8,128)(2,1)S(1)}, u32[]{:S(2)}, u32[]{:S(2)}) collective-permute-start(bf16[256,512]{1,0:T(8,128)(2,1)S(1)} %multiply_convert_fusion.13), channel_id=1, source_target_pairs={{0,1},{1,2},{2,3},{3,4},{4,5},{5,6},{6,7},{7,8},{8,9},{9,10},{10,1... | collective-permute-start | bytes 786440 | tf_op jit(solution)/shard_map/ppermute | solution.py:13
  65.3 12.3 %collective-permute-start.10 = (bf16[256,512]{1,0:T(8,128)(2,1)S(1)}, bf16[256,512]{1,0:T(8,128)(2,1)S(1)}, u32[]{:S(2)}, u32[]{:S(2)}) collective-permute-start(bf16[256,512]{1,0:T(8,128)(2,1)S(1)} %multiply_convert_fusion.13), channel_id=1, source_target_pairs={{0,63},{1,0},{2,1},{3,2},{4,3},{5,4},{6,5},{7,6},{8,7},{9,8},{10,9... | collective-permute-start | bytes 786440 | tf_op jit(solution)/shard_map/ppermute | solution.py:13
  67.9 9.7 %collective-permute-start.11 = (bf16[256,512]{1,0:T(8,128)(2,1)S(1)}, bf16[256,512]{1,0:T(8,128)(2,1)S(1)}, u32[]{:S(2)}, u32[]{:S(2)}) collective-permute-start(bf16[256,512]{1,0:T(8,128)(2,1)S(1)} %multiply_convert_fusion.13), channel_id=1, source_target_pairs={{0,62},{1,63},{2,0},{3,1},{4,2},{5,3},{6,4},{7,5},{8,6},{9,7},{10,... | collective-permute-start | bytes 786440 | tf_op jit(solution)/shard_map/ppermute | solution.py:13
  75.0 2.7 %copy-start.8 = (bf16[2,512,512]{2,1,0:T(8,128)(2,1)S(1)}, bf16[2,512,512]{2,1,0:T(8,128)(2,1)}, u32[]{:S(2)}) copy-start(bf16[2,512,512]{2,1,0:T(8,128)(2,1)} %param.36) | copy-start | bytes 3145732
  120.3 2.2 copy-start.7
  122.2 10.5 %copy-start.3 = (f32[256,512]{1,0:T(8,128)}, f32[256,512]{1,0:T(8,128)S(1)}, u32[]{:S(2)}) copy-start(f32[256,512]{1,0:T(8,128)S(1)} %get-tuple-element.147) | copy-start | bytes 1572868
  122.4 10.3 %collective-permute-start.12 = (bf16[256,512]{1,0:T(8,128)(2,1)S(1)}, bf16[256,512]{1,0:T(8,128)(2,1)S(1)}, u32[]{:S(2)}, u32[]{:S(2)}) collective-permute-start(bf16[256,512]{1,0:T(8,128)(2,1)S(1)} %multiply_convert_fusion.8), channel_id=1, source_target_pairs={{0,2},{1,3},{2,4},{3,5},{4,6},{5,7},{6,8},{7,9},{8,10},{9,11},{10,... | collective-permute-start | bytes 786440 | tf_op jit(solution)/shard_map/ppermute | solution.py:13
  122.5 10.2 %collective-permute-start.13 = (bf16[256,512]{1,0:T(8,128)(2,1)S(1)}, bf16[256,512]{1,0:T(8,128)(2,1)S(1)}, u32[]{:S(2)}, u32[]{:S(2)}) collective-permute-start(bf16[256,512]{1,0:T(8,128)(2,1)S(1)} %multiply_convert_fusion.8), channel_id=1, source_target_pairs={{0,1},{1,2},{2,3},{3,4},{4,5},{5,6},{6,7},{7,8},{8,9},{9,10},{10,1... | collective-permute-start | bytes 786440 | tf_op jit(solution)/shard_map/ppermute | solution.py:13
  122.6 10.3 %collective-permute-start.14 = (bf16[256,512]{1,0:T(8,128)(2,1)S(1)}, bf16[256,512]{1,0:T(8,128)(2,1)S(1)}, u32[]{:S(2)}, u32[]{:S(2)}) collective-permute-start(bf16[256,512]{1,0:T(8,128)(2,1)S(1)} %multiply_convert_fusion.8), channel_id=1, source_target_pairs={{0,63},{1,0},{2,1},{3,2},{4,3},{5,4},{6,5},{7,6},{8,7},{9,8},{10,9... | collective-permute-start | bytes 786440 | tf_op jit(solution)/shard_map/ppermute | solution.py:13
  125.5 9.5 %collective-permute-start.15 = (bf16[256,512]{1,0:T(8,128)(2,1)S(1)}, bf16[256,512]{1,0:T(8,128)(2,1)S(1)}, u32[]{:S(2)}, u32[]{:S(2)}) collective-permute-start(bf16[256,512]{1,0:T(8,128)(2,1)S(1)} %multiply_convert_fusion.8), channel_id=1, source_target_pairs={{0,62},{1,63},{2,0},{3,1},{4,2},{5,3},{6,4},{7,5},{8,6},{9,7},{10,... | collective-permute-start | bytes 786440 | tf_op jit(solution)/shard_map/ppermute | solution.py:13
  132.7 2.3 %copy-start.9 = (bf16[2,512,512]{2,1,0:T(8,128)(2,1)S(1)}, bf16[2,512,512]{2,1,0:T(8,128)(2,1)}, u32[]{:S(2)}) copy-start(bf16[2,512,512]{2,1,0:T(8,128)(2,1)} %param.36) | copy-start | bytes 3145732
  185.9 2.2 copy-start.1
  185.9 2.2 copy-start.4
  188.1 16.8 %collective-permute-start.16 = (bf16[512,512]{1,0:T(8,128)(2,1)}, bf16[512,512]{1,0:T(8,128)(2,1)}, u32[]{:S(2)}, u32[]{:S(2)}) collective-permute-start(bf16[512,512]{1,0:T(8,128)(2,1)} %get-tuple-element.126), channel_id=1, source_target_pairs={{0,2},{1,3},{2,4},{3,5},{4,6},{5,7},{6,8},{7,9},{8,10},{9,11},{10,... | collective-permute-start | bytes 1572872 | tf_op jit(solution)/shard_map/ppermute | solution.py:13
  188.1 18.7 %collective-permute-start.17 = (bf16[512,512]{1,0:T(8,128)(2,1)}, bf16[512,512]{1,0:T(8,128)(2,1)}, u32[]{:S(2)}, u32[]{:S(2)}) collective-permute-start(bf16[512,512]{1,0:T(8,128)(2,1)} %get-tuple-element.125), channel_id=1, source_target_pairs={{0,1},{1,2},{2,3},{3,4},{4,5},{5,6},{6,7},{7,8},{8,9},{9,10},{10,1... | collective-permute-start | bytes 1572872 | tf_op jit(solution)/shard_map/ppermute | solution.py:13
  191.2 17.8 %collective-permute-start.18 = (bf16[512,512]{1,0:T(8,128)(2,1)}, bf16[512,512]{1,0:T(8,128)(2,1)S(1)}, u32[]{:S(2)}, u32[]{:S(2)}) collective-permute-start(bf16[512,512]{1,0:T(8,128)(2,1)} %get-tuple-element.124), channel_id=1, source_target_pairs={{0,63},{1,0},{2,1},{3,2},{4,3},{5,4},{6,5},{7,6},{8,7},{9,8},{10,9... | collective-permute-start | bytes 1572872 | tf_op jit(solution)/shard_map/ppermute | solution.py:13
  194.1 18.3 %collective-permute-start.19 = (bf16[512,512]{1,0:T(8,128)(2,1)}, bf16[512,512]{1,0:T(8,128)(2,1)S(1)}, u32[]{:S(2)}, u32[]{:S(2)}) collective-permute-start(bf16[512,512]{1,0:T(8,128)(2,1)} %get-tuple-element.123), channel_id=1, source_target_pairs={{0,62},{1,63},{2,0},{3,1},{4,2},{5,3},{6,4},{7,5},{8,6},{9,7},{10,... | collective-permute-start | bytes 1572872 | tf_op jit(solution)/shard_map/ppermute | solution.py:13
  217.5 3.4 %copy-start.5 = (bf16[512,128]{1,0:T(8,128)(2,1)S(1)}, bf16[512,128]{1,0:T(8,128)(2,1)}, u32[]{:S(2)}) copy-start(bf16[512,128]{1,0:T(8,128)(2,1)} %param.45) | copy-start | bytes 393220
  (3 other events, 5.7 us)
where the time goes:
time: 225 us; the launch traced here: 222 us
  matrix products  76.9 us (34%)
  local copies, waits for them, and re-layouts  58.3 us (26%)
  starting transfers between devices  44.7 us (20%)
  waiting for transfers between devices  28.1 us (12%)
  other arithmetic  12.8 us (6%)
    ppermute x20, starting transfers between devices, shifted(): return lax.ppermute(value, axis, pairs)  44.7 us
    ppermute x20, waiting for transfers between devices, shifted(): return lax.ppermute(value, axis, pairs)  28.1 us
    dot_general x16, matrix products, single(): jnp.dot(softmax_weights, value_head, preferred_element_type=jnp.float32)  23 us
    dot_general x16, matrix products, single(): lax.dot_general(query_head, key_head, (((1,), (1,)), ((), ())), preferred...  20 us
    broadcast_in_dim x32, local copies, waits for them, and re-layouts, single(): jnp.where(allowed[:, :, None], scores.reshape(row_count, 5, -1), -jnp.inf)  8.05 us
    gather x1, local copies, waits for them, and re-layouts, body(): answer_rows = decoded[jnp.clip(arrived, 0, mesh_rows - 1)]  7.66 us
    reshape x2, local copies, waits for them, and re-layouts, attend(): values_near = value_rows.reshape(-1, HEADS, head_dim).transpose(1, 0, 2)  7.5 us
    dot_general x2, matrix products, grid_mlp(): jnp.dot(grid_hidden, w_grid, preferred_element_type=jnp.float32)  6.89 us
  transfers between devices with their start and end apart: 20, of which 11 were waited for; matrix products, arithmetic and copies ran while one was open for 9% of the time, Pallas kernels for 0%

commit v1 on v0

v1 whole, which is shorter than its diff:
```python
import functools

import jax
import jax.numpy as jnp
from jax import lax
from jax.experimental import pallas as pl
from jax.experimental.pallas import tpu as pltpu
from jax.sharding import PartitionSpec as P

HEADS = 8
LAYERS = 2
PAIRS = HEADS // 2
HALVES = 2
BIG = 1e30
MESH = pl.DeviceIdType.MESH
F32 = jnp.float32
BF16 = jnp.bfloat16


def dot(left, right):
    return jnp.dot(left, right, preferred_element_type=F32)


def dot_t(left, right):
    return lax.dot_general(left, right, (((1,), (1,)), ((), ())), preferred_element_type=F32)


def silu(v):
    return v * (0.5 + 0.5 * jnp.tanh(0.5 * v))


def rms(values, gain):
    return values * lax.rsqrt(jnp.mean(values * values, axis=-1, keepdims=True) + 1e-06) * gain


def to_columns(row, lanes=128):
    return jnp.broadcast_to(row, (lanes, row.shape[1])).T


def kernel(
    count,
    grid_in,
    dest_block,
    dest_node,
    mask_in,
    mesh_embed,
    w_in,
    in_bias,
    w_grid,
    w_enc,
    attn_gain,
    w_query,
    w_key,
    w_value,
    w_out,
    mlp_gain,
    w_up,
    w_down,
    dec_gain,
    w_dec,
    w_head,
    w_final,
    out,
    v_grid,
    v_db,
    v_dn,
    v_mask,
    v_embed,
    v_win,
    v_bias,
    v_wgrid,
    v_wenc,
    v_again,
    v_wq,
    v_wk,
    v_wv,
    v_wo,
    v_mgain,
    v_wu,
    v_wd,
    v_dgain,
    v_wdec,
    v_whead,
    v_wfinal,
    feat,
    psend,
    csend,
    crecv,
    erecv,
    pown,
    pnear,
    state,
    bias,
    xs,
    rx,
    q_scr,
    k_scr,
    v_scr,
    m_scr,
    r_scr,
    att,
    gather,
    acc,
    obuf,
    load_sem,
    es_sem,
    er_sem,
    xs_sem,
    xr_sem,
    out_sem,
):
    me = lax.axis_index("block")
    core = lax.rem(me, 2)
    side = 2 * core - 1
    grid_rows, _ = grid_in.shape
    mesh_rows, width = mesh_embed.shape
    half = mesh_rows // HALVES

    def device(offset):
        return {"block": lax.rem(me + offset + count, count)}

    barrier = pltpu.get_barrier_semaphore()
    for offset in (-2, -1, 1, 2):
        pl.semaphore_signal(barrier, inc=1, device_id=device(offset), device_id_type=MESH)

    sources = (
        grid_in, dest_block, dest_node, w_in, in_bias, w_grid, mask_in, mesh_embed, w_enc, attn_gain,
        w_query, w_key, w_value, w_out, mlp_gain, w_up, w_down, dec_gain, w_dec, w_head, w_final,
    )
    targets = (
        v_grid, v_db, v_dn, v_win, v_bias, v_wgrid, v_mask, v_embed, v_wenc, v_again,
        v_wq, v_wk, v_wv, v_wo, v_mgain, v_wu, v_wd, v_dgain, v_wdec, v_whead, v_wfinal,
    )
    loads = {}
    for index, (source, target) in enumerate(zip(sources, targets)):
        copy = pltpu.make_async_copy(source, target, load_sem.at[index])
        copy.start()
        loads[index] = copy

    def need(*refs):
        for index, target in enumerate(targets):
            if any(target is ref for ref in refs) and index in loads:
                loads.pop(index).wait()

    started = []

    def send(src, dst, s_sem, r_sem, offset):
        copy = pltpu.make_async_remote_copy(
            src_ref=src,
            dst_ref=dst,
            send_sem=s_sem,
            recv_sem=r_sem,
            device_id=device(offset),
            device_id_type=MESH,
        )
        copy.start()
        started.append(copy)
        return copy

    need(v_grid, v_win, v_bias, v_wgrid, v_db, v_dn)
    in_row = v_bias[...].astype(F32)
    for step in range(grid_rows // mesh_rows):
        rows = pl.ds(step * mesh_rows, mesh_rows)
        hidden = silu(dot(v_grid[rows, :], v_win[...]) + in_row).astype(BF16)
        feat[rows, :] = dot(hidden, v_wgrid[...]).astype(BF16)

    relative = v_db[...] - me
    relative = jnp.where(relative > count // 2, relative - count, relative)
    relative = jnp.where(relative < -(count // 2), relative + count, relative)
    code = relative * mesh_rows + v_dn[...]
    ones = jnp.ones((8, grid_rows), BF16)

    def partial(k):
        nodes = lax.broadcasted_iota(jnp.int32, (mesh_rows, grid_rows), 0) + k * side * mesh_rows
        match = jnp.where(nodes == code, 1.0, 0.0).astype(BF16)
        return dot(match, feat[...]), dot_t(ones, match)

    hrows = [pl.ds(h * half, half) for h in range(HALVES)]
    enc = {}

    def enc_send(name, index, slot, h, offset):
        enc[name] = send(
            psend.at[slot, hrows[h], :],
            erecv.at[slot, hrows[h], :],
            es_sem.at[index],
            er_sem.at[index],
            offset,
        )

    def count_send(index, counts, offset):
        csend[index] = counts
        enc[("count", index)] = send(
            csend.at[index], crecv.at[index], es_sem.at[8 + index], er_sem.at[8 + index], offset
        )

    sums, counts = partial(-2)
    psend[0] = sums.astype(BF16)
    pl.semaphore_wait(barrier, 4)
    for h in range(HALVES):
        enc_send(("combine", h), h, 0, h, -side)
    count_send(0, counts, -2 * side)
    sums, counts = partial(2)
    psend[1] = sums.astype(BF16)
    enc_send(("far", 0), 2, 1, 0, 2 * side)
    count_send(1, counts, 2 * side)
    sums, counts = partial(1)
    pnear[...] = sums
    count_send(3, counts, side)
    for h in range(HALVES):
        enc[("combine", h)].wait_recv()
        psend[3, hrows[h], :] = (pnear[hrows[h], :] + erecv[0, hrows[h], :].astype(F32)).astype(BF16)
        enc_send(("near", h), 4 + h, 3, h, side)
        if h == 0:
            enc_send(("far", 1), 3, 1, 1, 2 * side)
    sums, counts = partial(-1)
    psend[2] = sums.astype(BF16)
    for h in range(HALVES):
        enc_send(("partner", h), 6 + h, 2, h, -side)
    count_send(2, counts, -side)
    sums, own_counts = partial(0)
    pown[...] = sums

    code_columns = to_columns(code.astype(F32))
    lane = lax.broadcasted_iota(jnp.int32, (1, mesh_rows), 1).astype(F32)
    code_wide = jnp.concatenate([code_columns, code_columns], axis=1)
    base = (side * mesh_rows).astype(F32)
    for slot, k in enumerate((0, -1, -2, 2, 1)):
        gather[slot] = jnp.where(code_wide == lane + k * base, 1.0, 0.0).astype(BF16)

    need(v_mask)
    columns = [to_columns(v_mask[pl.ds(c, 1), :].astype(F32)) for c in range(4)]
    minus = jnp.zeros((mesh_rows, 128), F32) + core.astype(F32) > 0.5
    by_slot = (
        jnp.where(minus, columns[1], columns[2]),
        jnp.where(minus, columns[0], columns[3]),
        jnp.where(minus, columns[3], columns[0]),
        jnp.where(minus, columns[2], columns[1]),
    )
    for slot, value in enumerate(by_slot):
        bias[slot] = jnp.where(value > 0.5, 0.0, BIG)

    far_sends = {}

    def broadcast(phase, h):
        for slot, offset in ((0, -side), (1, 2 * side), (2, -2 * side)):
            far_sends[phase, slot, h] = send(
                xs.at[phase, hrows[h], :],
                rx.at[phase, slot, hrows[h], :],
                xs_sem.at[phase, slot, h],
                xr_sem.at[phase, slot, h],
                offset,
            )

    def forward(phase, h):
        far_sends[phase, 1, h].wait_recv()
        far_sends[phase, 3, h] = send(
            rx.at[phase, 1, hrows[h], :],
            rx.at[phase, 3, hrows[h], :],
            xs_sem.at[phase, 3, h],
            xr_sem.at[phase, 3, h],
            -side,
        )

    need(v_embed, v_wenc, v_again)
    for index in range(4):
        enc[("count", index)].wait_recv()
    total = own_counts + crecv[0] + crecv[1] + crecv[2] + crecv[3]
    scale = to_columns(1.0 / jnp.maximum(total[0:1, :], 1.0))
    scale = jnp.concatenate([scale] * (width // 128), axis=1)
    for h in range(HALVES):
        rows = hrows[h]
        for name in ("partner", "far", "near"):
            enc[(name, h)].wait_recv()
        summed = pown[rows, :] + erecv[1, rows, :].astype(F32)
        summed = summed + erecv[2, rows, :].astype(F32) + erecv[3, rows, :].astype(F32)
        mean_rows = (summed * scale[h * half : (h + 1) * half]).astype(BF16)
        value = v_embed[rows, :].astype(F32) + dot(mean_rows, v_wenc[...])
        state[rows, :] = value
        xs[0, rows, :] = rms(value, v_again[pl.ds(0, 1), :].astype(F32)).astype(BF16)
        broadcast(0, h)

    low = lax.broadcasted_iota(jnp.int32, (1, 128), 1) < 64

    def project(layer, slot, value):
        keys = dot(value, v_wk[layer])
        values = dot(value, v_wv[layer])
        for j in range(PAIRS):
            cut = slice(j * 128, (j + 1) * 128)
            k_scr[slot, j] = keys[:, cut].astype(BF16)
            v_scr[slot, 2 * j] = jnp.where(low, values[:, cut], 1.0).astype(BF16)
            v_scr[slot, 2 * j + 1] = jnp.where(low, 1.0, values[:, cut]).astype(BF16)

    def group(h, j, rows, slots, start):
        query = q_scr[h, rows, :]
        scores = [dot_t(query, k_scr[slot, j]) for slot in slots]
        best = start
        for slot, score in zip(slots, scores):
            top = jnp.maximum(score[:, :128], score[:, 128:])
            if slot:
                top = top - bias[slot - 1, rows, :]
            best = top if best is None else jnp.maximum(best, top)
        best = jnp.broadcast_to(jnp.max(best, axis=-1, keepdims=True), best.shape)
        result = None
        for slot, score in zip(slots, scores):
            shift = best + bias[slot - 1, rows, :] if slot else best
            weights = jnp.exp(score - jnp.concatenate([shift, shift], axis=1)).astype(BF16)
            term = dot(weights, v_scr[slot, h])
            result = term if result is None else result + term
        return best, result

    for layer in range(LAYERS):
        need(v_wq, v_wk, v_wv)
        value = xs[layer]
        queries = dot(value, v_wq[layer]) * 0.125
        for j in range(PAIRS):
            cut = queries[:, j * 128 : (j + 1) * 128]
            q_scr[2 * j] = jnp.where(low, cut, 0.0).astype(BF16)
            q_scr[2 * j + 1] = jnp.where(low, 0.0, cut).astype(BF16)
        project(layer, 0, value)
        for h in range(HALVES):
            far_sends[layer, 0, h].wait_recv()
        project(layer, 1, rx[layer, 0])
        everything = pl.ds(0, mesh_rows)

        def first(h):
            for odd in range(2):
                best, result = group(2 * h + odd, h, everything, (0, 1), None)
                m_scr[2 * h + odd] = best
                r_scr[2 * h + odd] = result

        for j in range(PAIRS):
            first(j)
            if j % 2 == 1:
                forward(layer, j // 2)
        for slot in (1, 2, 3):
            for h in range(HALVES):
                if slot > 1:
                    far_sends[layer, slot, h].wait_recv()
            project(layer, slot + 1, rx[layer, slot])
        need(v_wo, v_mgain, v_wu, v_wd, v_dgain, v_wdec)
        for h in range(HALVES):
            rows = hrows[h]
            for j in range(PAIRS):
                parts = []
                for odd in range(2):
                    head = 2 * j + odd
                    before = m_scr[head, rows, :]
                    best, result = group(head, j, rows, (2, 3, 4), before)
                    parts.append(r_scr[head, rows, :] * jnp.exp(before - best) + result)
                top = jnp.where(low, parts[0], parts[1])
                bottom = pltpu.roll(jnp.where(low, parts[1], parts[0]), 64, 1)
                att[rows, pl.ds(j * 128, 128)] = (top / bottom).astype(BF16)
            value = state[rows, :] + dot(att[rows, :], v_wo[layer])
            normed = rms(value, v_mgain[pl.ds(layer, 1), :].astype(F32)).astype(BF16)
            up = silu(dot(normed, v_wu[layer])).astype(BF16)
            value = value + dot(up, v_wd[layer])
            if layer + 1 < LAYERS:
                state[rows, :] = value
                sent = rms(value, v_again[pl.ds(layer + 1, 1), :].astype(F32)).astype(BF16)
            else:
                decoded = rms(value, v_dgain[...].astype(F32)).astype(BF16)
                sent = dot(decoded, v_wdec[...]).astype(BF16)
            xs[layer + 1, rows, :] = sent
            broadcast(layer + 1, h)

    steps = grid_rows // mesh_rows
    for h in range(HALVES):
        far_sends[LAYERS, 0, h].wait_recv()
    for step in range(steps):
        rows = pl.ds(step * mesh_rows, mesh_rows)
        acc[rows, :] = (
            feat[rows, :].astype(F32)
            + dot(gather[0, rows, :], xs[LAYERS])
            + dot(gather[1, rows, :], rx[LAYERS, 0])
        )
        if step % 2 == 1:
            forward(LAYERS, step // 2)
    for h in range(HALVES):
        far_sends[LAYERS, 2, h].wait_recv()
    for step in range(steps):
        rows = pl.ds(step * mesh_rows, mesh_rows)
        acc[rows, :] = (
            acc[rows, :]
            + dot(gather[2, rows, :], rx[LAYERS, 1])
            + dot(gather[3, rows, :], rx[LAYERS, 2])
        )
    for h in range(HALVES):
        far_sends[LAYERS, 3, h].wait_recv()
    need(v_whead, v_wfinal)
    writes = []
    for step in range(steps):
        rows = pl.ds(step * mesh_rows, mesh_rows)
        mixed = (acc[rows, :] + dot(gather[4, rows, :], rx[LAYERS, 3])).astype(BF16)
        head_rows = silu(dot(mixed, v_whead[...])).astype(BF16)
        obuf[rows, :] = dot(head_rows, v_wfinal[...]).astype(BF16)
        copy = pltpu.make_async_copy(obuf.at[rows, :], out.at[rows, :], out_sem.at[step])
        copy.start()
        writes.append(copy)
    for copy in started:
        copy.wait_send()
    for copy in writes:
        copy.wait()


def body(
    grid_in, dest_block, dest_node, neighbour_mask, mesh_embed, w_in, in_bias, w_grid, w_enc, attn_gain,
    w_query, w_key, w_value, w_out, mlp_gain, w_up, w_down, dec_gain, w_dec, w_head, w_final,
):
    count = lax.axis_size("block")
    grid_rows, channels = grid_in.shape
    mesh_rows, width = mesh_embed.shape
    operands = [
        grid_in,
        dest_block.reshape(1, grid_rows),
        dest_node.reshape(1, grid_rows),
        neighbour_mask.T,
        mesh_embed,
        w_in,
        in_bias.reshape(1, width),
        w_grid,
        w_enc,
        attn_gain,
        w_query,
        w_key,
        w_value,
        w_out,
        mlp_gain,
        w_up,
        w_down,
        dec_gain.reshape(1, width),
        w_dec,
        w_head,
        w_final,
    ]
    phases = LAYERS + 1
    scratch = [pltpu.VMEM(operand.shape, operand.dtype) for operand in operands] + [
        pltpu.VMEM((grid_rows, width), BF16),
        pltpu.VMEM((4, mesh_rows, width), BF16),
        pltpu.VMEM((4, 8, mesh_rows), F32),
        pltpu.VMEM((4, 8, mesh_rows), F32),
        pltpu.VMEM((4, mesh_rows, width), BF16),
        pltpu.VMEM((mesh_rows, width), F32),
        pltpu.VMEM((mesh_rows, width), F32),
        pltpu.VMEM((mesh_rows, width), F32),
        pltpu.VMEM((4, mesh_rows, 128), F32),
        pltpu.VMEM((phases, mesh_rows, width), BF16),
        pltpu.VMEM((phases, 4, mesh_rows, width), BF16),
        pltpu.VMEM((HEADS, mesh_rows, 128), BF16),
        pltpu.VMEM((5, PAIRS, mesh_rows, 128), BF16),
        pltpu.VMEM((5, HEADS, mesh_rows, 128), BF16),
        pltpu.VMEM((HEADS, mesh_rows, 128), F32),
        pltpu.VMEM((HEADS, mesh_rows, 128), F32),
        pltpu.VMEM((mesh_rows, width), BF16),
        pltpu.VMEM((5, grid_rows, mesh_rows), BF16),
        pltpu.VMEM((grid_rows, width), F32),
        pltpu.VMEM((grid_rows, channels), BF16),
        pltpu.SemaphoreType.DMA((len(operands),)),
        pltpu.SemaphoreType.DMA((12,)),
        pltpu.SemaphoreType.DMA((12,)),
        pltpu.SemaphoreType.DMA((phases, 4, HALVES)),
        pltpu.SemaphoreType.DMA((phases, 4, HALVES)),
        pltpu.SemaphoreType.DMA((grid_rows // mesh_rows,)),
    ]
    return pl.pallas_call(
        functools.partial(kernel, count),
        out_shape=jax.ShapeDtypeStruct((grid_rows, channels), BF16),
        in_specs=[pl.BlockSpec(memory_space=pl.ANY)] * len(operands),
        out_specs=pl.BlockSpec(memory_space=pl.ANY),
        scratch_shapes=scratch,
        compiler_params=pltpu.CompilerParams(
            collective_id=0, has_side_effects=True, vmem_limit_bytes=60 * 1024 * 1024
        ),
        name="step",
    )(*operands)


def solution(mesh):
    rows = P(("member", "block"), None)
    placed = (rows, rows, P(("member", "block")), rows, rows) + (P(),) * 16
    return jax.shard_map(body, mesh=mesh, in_specs=placed, out_specs=rows, check_vma=False)
```

time: 225 us -> 75.8 us (0.34)
  the two profiles are of different devices: /device:TPU:46 before, /device:TPU:37 now
where the time goes in v1:
time: 75.8 us; the launch traced here: 75.6 us
  Pallas kernels  72 us (95%)
  local copies, waits for them, and re-layouts  3.62 us (5%)
    pallas_call x1, Pallas kernels, body(): pl.pallas_call(functools.partial(kernel, count), out_shape=jax.ShapeDtype...  72 us
    unnamed x5, local copies, waits for them, and re-layouts  2.45 us

profile of v1, /device:TPU:37, one launch (start us, length us, event | category | flops | bytes accessed | tf_op | source)
XLA Modules:
  0.0 75.6 jit_solution(17928424679192940963)
XLA Ops:
  0.0 0.0 copy-start
  0.0 0.7 copy-done
  0.7 0.0 copy-start.1
  0.7 0.6 reshape.14.in_bias
  1.3 0.1 copy-done.1
  1.4 0.6 reshape.15.dec_gain
  2.0 72.0 %step.1 = bf16[1024,128]{1,0:T(8,128)(2,1)} custom-call(bf16[1024,128]{1,0:T(8,128)(2,1)} %grid_in.1, s32[1,1024]{1,0:T(1,128)} %bitcast.3, s32[1,1024]{1,0:T(1,128)} %bitcast.4, s32[4,256]{1,0:T(4,128)} %bitcast.5, bf16[256,512]{1,0:T(8,128)(2,1)} %mesh_embed.1, bf16[128,512]{1,0:T(8,128)(2,1)} %w_in.1, bf16[1,512]{1,0:T(2,128)(2,1)} %reshape.14.in_bias, ...), custom_call_target="tpu_custom_call" | custom-call | tf_op jit(solution)/shard_map/step/pallas_call | solution.py:464
  73.9 1.7 %copy.23 = bf16[1024,128]{1,0:T(8,128)(2,1)} copy(bf16[1024,128]{1,0:T(8,128)(2,1)} %step.1) | data formatting | bytes 524288
Async XLA Ops:
  0.0 0.7 copy-start
  0.7 0.7 copy-start.1

commit v2 on v1

--- a/solution.py
+++ b/solution.py
@@ -31,6 +31,11 @@
 
 def rms(values, gain):
     return values * lax.rsqrt(jnp.mean(values * values, axis=-1, keepdims=True) + 1e-06) * gain
+
+
+def as_row(ref):
+    value = ref[...].astype(F32)
+    return jnp.concatenate([value[i : i + 1] for i in range(value.shape[0])], axis=1)
 
 
 def to_columns(row, lanes=128):
@@ -101,13 +106,11 @@
     att,
     gather,
     acc,
-    obuf,
     load_sem,
     es_sem,
     er_sem,
     xs_sem,
     xr_sem,
-    out_sem,
 ):
     me = lax.axis_index("block")
     core = lax.rem(me, 2)
@@ -132,10 +135,14 @@
         v_wq, v_wk, v_wv, v_wo, v_mgain, v_wu, v_wd, v_dgain, v_wdec, v_whead, v_wfinal,
     )
     loads = {}
-    for index, (source, target) in enumerate(zip(sources, targets)):
-        copy = pltpu.make_async_copy(source, target, load_sem.at[index])
-        copy.start()
-        loads[index] = copy
+
+    def load(first, last):
+        for index in range(first, last):
+            copy = pltpu.make_async_copy(sources[index], targets[index], load_sem.at[index])
+            copy.start()
+            loads[index] = copy
+
+    load(0, 6)
 
     def need(*refs):
         for index, target in enumerate(targets):
@@ -158,7 +165,8 @@
         return copy
 
     need(v_grid, v_win, v_bias, v_wgrid, v_db, v_dn)
-    in_row = v_bias[...].astype(F32)
+    load(6, len(sources))
+    in_row = as_row(v_bias)
     for step in range(grid_rows // mesh_rows):
         rows = pl.ds(step * mesh_rows, mesh_rows)
         hidden = silu(dot(v_grid[rows, :], v_win[...]) + in_row).astype(BF16)
@@ -224,8 +232,16 @@
     lane = lax.broadcasted_iota(jnp.int32, (1, mesh_rows), 1).astype(F32)
     code_wide = jnp.concatenate([code_columns, code_columns], axis=1)
     base = (side * mesh_rows).astype(F32)
-    for slot, k in enumerate((0, -1, -2, 2, 1)):
-        gather[slot] = jnp.where(code_wide == lane + k * base, 1.0, 0.0).astype(BF16)
+    left = lane < half
+    wanted = (
+        lane,
+        lane - base,
+        lane - 2 * base,
+        jnp.where(left, lane + 2 * base, lane - half + base),
+        jnp.where(left, lane + half + 2 * base, lane + base),
+    )
+    for tile, node in enumerate(wanted):
+        gather[tile] = jnp.where(code_wide == node, 1.0, 0.0).astype(BF16)
 
     need(v_mask)
     columns = [to_columns(v_mask[pl.ds(c, 1), :].astype(F32)) for c in range(4)]
@@ -241,25 +257,33 @@
 
     far_sends = {}
 
+    tile_rows = (pl.ds(0, half), pl.ds(half, half))
+
+    def far_send(phase, name, h, source, slot, rows, offset):
+        index = ("partner", "ahead", "behind", "passed").index(name)
+        far_sends[phase, name, h] = send(
+            source,
+            rx.at[phase, slot, rows, :],
+            xs_sem.at[phase, index, h],
+            xr_sem.at[phase, index, h],
+            offset,
+        )
+
     def broadcast(phase, h):
-        for slot, offset in ((0, -side), (1, 2 * side), (2, -2 * side)):
-            far_sends[phase, slot, h] = send(
-                xs.at[phase, hrows[h], :],
-                rx.at[phase, slot, hrows[h], :],
-                xs_sem.at[phase, slot, h],
-                xr_sem.at[phase, slot, h],
-                offset,
-            )
+        source = xs.at[phase, hrows[h], :]
+        far_send(phase, "ahead", h, source, 1, hrows[h], 2 * side)
+        far_send(phase, "partner", h, source, 0, hrows[h], -side)
+
+    def rest(phase, h):
+        far_send(phase, "behind", h, xs.at[phase, hrows[h], :], 2 + h, tile_rows[0], -2 * side)
 
     def forward(phase, h):
-        far_sends[phase, 1, h].wait_recv()
-        far_sends[phase, 3, h] = send(
-            rx.at[phase, 1, hrows[h], :],
-            rx.at[phase, 3, hrows[h], :],
-            xs_sem.at[phase, 3, h],
-            xr_sem.at[phase, 3, h],
-            -side,
-        )
+        far_sends[phase, "ahead", h].wait_recv()
+        far_send(phase, "passed", h, rx.at[phase, 1, hrows[h], :], 2 + h, tile_rows[1], -side)
+
+    def arrived(phase, name, *parts):
+        for h in parts:
+            far_sends[phase, name, h].wait_recv()
 
     need(v_embed, v_wenc, v_again)
     for index in range(4):
@@ -278,6 +302,7 @@
         state[rows, :] = value
         xs[0, rows, :] = rms(value, v_again[pl.ds(0, 1), :].astype(F32)).astype(BF16)
         broadcast(0, h)
+    rest(0, 0)
 
     low = lax.broadcasted_iota(jnp.int32, (1, 128), 1) < 64
 
@@ -290,23 +315,45 @@
             v_scr[slot, 2 * j] = jnp.where(low, values[:, cut], 1.0).astype(BF16)
             v_scr[slot, 2 * j + 1] = jnp.where(low, 1.0, values[:, cut]).astype(BF16)
 
-    def group(h, j, rows, slots, start):
-        query = q_scr[h, rows, :]
-        scores = [dot_t(query, k_scr[slot, j]) for slot in slots]
+    mask_of = {1: (0, 0), 2: (1, 1), 3: (2, 3), 4: (2, 3)}
+
+    def group(head, rows, tiles, start):
+        query = q_scr[head, rows, :]
+        scores = [dot_t(query, k_scr[tile, head // 2]) for tile in tiles]
         best = start
-        for slot, score in zip(slots, scores):
-            top = jnp.maximum(score[:, :128], score[:, 128:])
-            if slot:
-                top = top - bias[slot - 1, rows, :]
+        for tile, score in zip(tiles, scores):
+            sides = [score[:, :128], score[:, 128:]]
+            if tile and mask_of[tile][0] == mask_of[tile][1]:
+                top = jnp.maximum(*sides) - bias[mask_of[tile][0], rows, :]
+            elif tile:
+                top = jnp.maximum(*(x - bias[m, rows, :] for x, m in zip(sides, mask_of[tile])))
+            else:
+                top = jnp.maximum(*sides)
             best = top if best is None else jnp.maximum(best, top)
         best = jnp.broadcast_to(jnp.max(best, axis=-1, keepdims=True), best.shape)
         result = None
-        for slot, score in zip(slots, scores):
-            shift = best + bias[slot - 1, rows, :] if slot else best
-            weights = jnp.exp(score - jnp.concatenate([shift, shift], axis=1)).astype(BF16)
-            term = dot(weights, v_scr[slot, h])
+        for tile, score in zip(tiles, scores):
+            if tile:
+                shift = jnp.concatenate([best + bias[m, rows, :] for m in mask_of[tile]], axis=1)
+            else:
+                shift = jnp.concatenate([best, best], axis=1)
+            weights = jnp.exp(score - shift).astype(BF16)
+            term = dot(weights, v_scr[tile, head])
             result = term if result is None else result + term
         return best, result
+
+    def merged(head, rows, tiles):
+        before = m_scr[head, rows, :]
+        best, result = group(head, rows, tiles, before)
+        return best, r_scr[head, rows, :] * jnp.exp(before - best) + result
+
+    everything = pl.ds(0, mesh_rows)
+
+    def absorb(tile):
+        for head in range(HEADS):
+            best, result = merged(head, everything, (tile,))
+            m_scr[head] = best
+            r_scr[head] = result
 
     for layer in range(LAYERS):
         need(v_wq, v_wk, v_wv)
@@ -317,39 +364,35 @@
             q_scr[2 * j] = jnp.where(low, cut, 0.0).astype(BF16)
             q_scr[2 * j + 1] = jnp.where(low, 0.0, cut).astype(BF16)
         project(layer, 0, value)
-        for h in range(HALVES):
-            far_sends[layer, 0, h].wait_recv()
+        arrived(layer, "partner", 0, 1)
         project(layer, 1, rx[layer, 0])
-        everything = pl.ds(0, mesh_rows)
-
-        def first(h):
-            for odd in range(2):
-                best, result = group(2 * h + odd, h, everything, (0, 1), None)
-                m_scr[2 * h + odd] = best
-                r_scr[2 * h + odd] = result
-
-        for j in range(PAIRS):
-            first(j)
-            if j % 2 == 1:
-                forward(layer, j // 2)
-        for slot in (1, 2, 3):
-            for h in range(HALVES):
-                if slot > 1:
-                    far_sends[layer, slot, h].wait_recv()
-            project(layer, slot + 1, rx[layer, slot])
+        for head in range(HEADS):
+            best, result = group(head, everything, (0, 1), None)
+            m_scr[head] = best
+            r_scr[head] = result
+            if head == 5:
+                forward(layer, 0)
+                rest(layer, 1)
+        arrived(layer, "behind", 0)
+        arrived(layer, "passed", 0)
+        project(layer, 3, rx[layer, 2])
+        absorb(3)
+        forward(layer, 1)
+        project(layer, 2, rx[layer, 1])
+        absorb(2)
+        arrived(layer, "behind", 1)
+        arrived(layer, "passed", 1)
+        project(layer, 4, rx[layer, 3])
         need(v_wo, v_mgain, v_wu, v_wd, v_dgain, v_wdec)
         for h in range(HALVES):
             rows = hrows[h]
             for j in range(PAIRS):
-                parts = []
-                for odd in range(2):
-                    head = 2 * j + odd
-                    before = m_scr[head, rows, :]
-                    best, result = group(head, j, rows, (2, 3, 4), before)
-                    parts.append(r_scr[head, rows, :] * jnp.exp(before - best) + result)
+                parts = [merged(2 * j + odd, rows, (4,))[1] for odd in range(2)]
                 top = jnp.where(low, parts[0], parts[1])
                 bottom = pltpu.roll(jnp.where(low, parts[1], parts[0]), 64, 1)
                 att[rows, pl.ds(j * 128, 128)] = (top / bottom).astype(BF16)
+            if h:
+                rest(layer + 1, 0)
             value = state[rows, :] + dot(att[rows, :], v_wo[layer])
             normed = rms(value, v_mgain[pl.ds(layer, 1), :].astype(F32)).astype(BF16)
             up = silu(dot(normed, v_wu[layer])).astype(BF16)
@@ -358,48 +401,45 @@
                 state[rows, :] = value
                 sent = rms(value, v_again[pl.ds(layer + 1, 1), :].astype(F32)).astype(BF16)
             else:
-                decoded = rms(value, v_dgain[...].astype(F32)).astype(BF16)
+                decoded = rms(value, as_row(v_dgain)).astype(BF16)
                 sent = dot(decoded, v_wdec[...]).astype(BF16)
             xs[layer + 1, rows, :] = sent
             broadcast(layer + 1, h)
 
     steps = grid_rows // mesh_rows
-    for h in range(HALVES):
-        far_sends[LAYERS, 0, h].wait_recv()
+    last = LAYERS
+
+    def add(tile, slot):
+        for step in range(steps):
+            rows = pl.ds(step * mesh_rows, mesh_rows)
+            acc[rows, :] = acc[rows, :] + dot(gather[tile, rows, :], rx[last, slot])
+
+    arrived(last, "partner", 0, 1)
     for step in range(steps):
         rows = pl.ds(step * mesh_rows, mesh_rows)
         acc[rows, :] = (
             feat[rows, :].astype(F32)
-            + dot(gather[0, rows, :], xs[LAYERS])
-            + dot(gather[1, rows, :], rx[LAYERS, 0])
+            + dot(gather[0, rows, :], xs[last])
+            + dot(gather[1, rows, :], rx[last, 0])
         )
-        if step % 2 == 1:
-            forward(LAYERS, step // 2)
-    for h in range(HALVES):
-        far_sends[LAYERS, 2, h].wait_recv()
+        if step == 1:
+            rest(last, 1)
+    forward(last, 0)
+    arrived(last, "behind", 0)
+    arrived(last, "passed", 0)
+    add(3, 2)
+    forward(last, 1)
+    add(2, 1)
+    need(v_whead, v_wfinal)
+    arrived(last, "behind", 1)
+    arrived(last, "passed", 1)
     for step in range(steps):
         rows = pl.ds(step * mesh_rows, mesh_rows)
-        acc[rows, :] = (
-            acc[rows, :]
-            + dot(gather[2, rows, :], rx[LAYERS, 1])
-            + dot(gather[3, rows, :], rx[LAYERS, 2])
-        )
-    for h in range(HALVES):
-        far_sends[LAYERS, 3, h].wait_recv()
-    need(v_whead, v_wfinal)
-    writes = []
-    for step in range(steps):
-        rows = pl.ds(step * mesh_rows, mesh_rows)
-        mixed = (acc[rows, :] + dot(gather[4, rows, :], rx[LAYERS, 3])).astype(BF16)
+        mixed = (acc[rows, :] + dot(gather[4, rows, :], rx[last, 3])).astype(BF16)
         head_rows = silu(dot(mixed, v_whead[...])).astype(BF16)
-        obuf[rows, :] = dot(head_rows, v_wfinal[...]).astype(BF16)
-        copy = pltpu.make_async_copy(obuf.at[rows, :], out.at[rows, :], out_sem.at[step])
-        copy.start()
-        writes.append(copy)
+        out[rows, :] = dot(head_rows, v_wfinal[...]).astype(BF16)
     for copy in started:
         copy.wait_send()
-    for copy in writes:
-        copy.wait()
 
 
 def body(
@@ -416,7 +456,7 @@
         neighbour_mask.T,
         mesh_embed,
         w_in,
-        in_bias.reshape(1, width),
+        in_bias.reshape(width // 128, 128),
         w_grid,
         w_enc,
         attn_gain,
@@ -427,7 +467,7 @@
         mlp_gain,
         w_up,
         w_down,
-        dec_gain.reshape(1, width),
+        dec_gain.reshape(width // 128, 128),
         w_dec,
         w_head,
         w_final,
@@ -453,19 +493,17 @@
         pltpu.VMEM((mesh_rows, width), BF16),
         pltpu.VMEM((5, grid_rows, mesh_rows), BF16),
         pltpu.VMEM((grid_rows, width), F32),
-        pltpu.VMEM((grid_rows, channels), BF16),
         pltpu.SemaphoreType.DMA((len(operands),)),
         pltpu.SemaphoreType.DMA((12,)),
         pltpu.SemaphoreType.DMA((12,)),
         pltpu.SemaphoreType.DMA((phases, 4, HALVES)),
         pltpu.SemaphoreType.DMA((phases, 4, HALVES)),
-        pltpu.SemaphoreType.DMA((grid_rows // mesh_rows,)),
     ]
     return pl.pallas_call(
         functools.partial(kernel, count),
         out_shape=jax.ShapeDtypeStruct((grid_rows, channels), BF16),
         in_specs=[pl.BlockSpec(memory_space=pl.ANY)] * len(operands),
-        out_specs=pl.BlockSpec(memory_space=pl.ANY),
+        out_specs=pl.BlockSpec(memory_space=pltpu.VMEM),
         scratch_shapes=scratch,
         compiler_params=pltpu.CompilerParams(
             collective_id=0, has_side_effects=True, vmem_limit_bytes=60 * 1024 * 1024

time: 75.8 us -> 69.1 us (0.912)
  Pallas kernels: 72 us -> 67.3 us
  local copies, waits for them, and re-layouts: 3.62 us -> 1.67 us
    pallas_call x1, Pallas kernels: 72 us -> 67.3 us  [body(): pl.pallas_call(functools.partial(kernel, count), out_shape=jax.ShapeDtype...]
    reshape x2 -> x0, local copies, waits for them, and re-layouts: 1.18 us -> none  [the longest x1 0.6 us: body(): dec_gain.reshape(1, width)]
    unnamed x5 -> x1, local copies, waits for them, and re-layouts: 2.45 us -> 1.67 us
where the time goes in v2:
time: 69.1 us; the launch traced here: 69 us
  Pallas kernels  67.3 us (97%)
  local copies, waits for them, and re-layouts  1.67 us (2%)
    pallas_call x1, Pallas kernels, body(): pl.pallas_call(functools.partial(kernel, count), out_shape=jax.ShapeDtype...  67.3 us
    unnamed x1, local copies, waits for them, and re-layouts  1.67 us

profile of v2, /device:TPU:37, one launch (start us, length us, event | category | flops | bytes accessed | tf_op | source)
XLA Modules:
  0.0 69.0 jit_solution(11969635563260684487)
XLA Ops:
  0.0 67.3 %step.1 = bf16[1024,128]{1,0:T(8,128)(2,1)} custom-call(bf16[1024,128]{1,0:T(8,128)(2,1)} %grid_in.1, s32[1,1024]{1,0:T(1,128)} %bitcast.5, s32[1,1024]{1,0:T(1,128)} %bitcast.6, s32[4,256]{1,0:T(4,128)} %bitcast.7, bf16[256,512]{1,0:T(8,128)(2,1)} %mesh_embed.1, bf16[128,512]{1,0:T(8,128)(2,1)} %w_in.1, bf16[4,128]{1,0:T(4,128)(2,1)} %bitcast.8, ...), custom_call_target="tpu_custom_call" | custom-call | tf_op jit(solution)/shard_map/step/pallas_call | solution.py:502
  67.3 1.7 %copy.23 = bf16[1024,128]{1,0:T(8,128)(2,1)} copy(bf16[1024,128]{1,0:T(8,128)(2,1)} %step.1) | data formatting | bytes 524288

commit v3 on v2

--- a/solution.py
+++ b/solution.py
@@ -12,6 +12,7 @@
 PAIRS = HEADS // 2
 HALVES = 2
 BIG = 1e30
+LOG2E = 1.4426950408889634
 MESH = pl.DeviceIdType.MESH
 F32 = jnp.float32
 BF16 = jnp.bfloat16
@@ -87,6 +88,7 @@
     v_wdec,
     v_whead,
     v_wfinal,
+    hidden,
     feat,
     psend,
     csend,
@@ -142,7 +144,7 @@
             copy.start()
             loads[index] = copy
 
-    load(0, 6)
+    load(0, 5)
 
     def need(*refs):
         for index, target in enumerate(targets):
@@ -164,13 +166,12 @@
         started.append(copy)
         return copy
 
-    need(v_grid, v_win, v_bias, v_wgrid, v_db, v_dn)
-    load(6, len(sources))
+    need(v_grid, v_win, v_bias, v_db, v_dn)
+    load(5, len(sources))
     in_row = as_row(v_bias)
     for step in range(grid_rows // mesh_rows):
         rows = pl.ds(step * mesh_rows, mesh_rows)
-        hidden = silu(dot(v_grid[rows, :], v_win[...]) + in_row).astype(BF16)
-        feat[rows, :] = dot(hidden, v_wgrid[...]).astype(BF16)
+        hidden[rows, :] = silu(dot(v_grid[rows, :], v_win[...]) + in_row).astype(BF16)
 
     relative = v_db[...] - me
     relative = jnp.where(relative > count // 2, relative - count, relative)
@@ -181,7 +182,7 @@
     def partial(k):
         nodes = lax.broadcasted_iota(jnp.int32, (mesh_rows, grid_rows), 0) + k * side * mesh_rows
         match = jnp.where(nodes == code, 1.0, 0.0).astype(BF16)
-        return dot(match, feat[...]), dot_t(ones, match)
+        return dot(match, hidden[...]), dot_t(ones, match)
 
     hrows = [pl.ds(h * half, half) for h in range(HALVES)]
     enc = {}
@@ -228,6 +229,11 @@
     sums, own_counts = partial(0)
     pown[...] = sums
 
+    need(v_wgrid)
+    for step in range(grid_rows // mesh_rows):
+        rows = pl.ds(step * mesh_rows, mesh_rows)
+        feat[rows, :] = dot(hidden[rows, :], v_wgrid[...]).astype(BF16)
+
     code_columns = to_columns(code.astype(F32))
     lane = lax.broadcasted_iota(jnp.int32, (1, mesh_rows), 1).astype(F32)
     code_wide = jnp.concatenate([code_columns, code_columns], axis=1)
@@ -252,8 +258,17 @@
         jnp.where(minus, columns[3], columns[0]),
         jnp.where(minus, columns[2], columns[1]),
     )
-    for slot, value in enumerate(by_slot):
-        bias[slot] = jnp.where(value > 0.5, 0.0, BIG)
+    lane_wide = lax.broadcasted_iota(jnp.int32, (1, 128), 1)
+    low = lane_wide < 64
+
+    def tag(odd, kind):
+        return jnp.where(lane_wide == kind + (0 if odd else 64), 1.0, 0.0)
+
+    for odd in range(2):
+        total = jnp.zeros((mesh_rows, 128), F32)
+        for kind, value in enumerate(by_slot):
+            total = total + jnp.where(value > 0.5, 0.0, -BIG) * tag(odd, kind)
+        bias[odd] = total
 
     far_sends = {}
 
@@ -297,55 +312,52 @@
             enc[(name, h)].wait_recv()
         summed = pown[rows, :] + erecv[1, rows, :].astype(F32)
         summed = summed + erecv[2, rows, :].astype(F32) + erecv[3, rows, :].astype(F32)
-        mean_rows = (summed * scale[h * half : (h + 1) * half]).astype(BF16)
+        mean_hidden = (summed * scale[h * half : (h + 1) * half]).astype(BF16)
+        mean_rows = dot(mean_hidden, v_wgrid[...]).astype(BF16)
         value = v_embed[rows, :].astype(F32) + dot(mean_rows, v_wenc[...])
         state[rows, :] = value
         xs[0, rows, :] = rms(value, v_again[pl.ds(0, 1), :].astype(F32)).astype(BF16)
         broadcast(0, h)
     rest(0, 0)
 
-    low = lax.broadcasted_iota(jnp.int32, (1, 128), 1) < 64
-
-    def project(layer, slot, value):
+    def project(layer, tile, value):
         keys = dot(value, v_wk[layer])
         values = dot(value, v_wv[layer])
-        for j in range(PAIRS):
-            cut = slice(j * 128, (j + 1) * 128)
-            k_scr[slot, j] = keys[:, cut].astype(BF16)
-            v_scr[slot, 2 * j] = jnp.where(low, values[:, cut], 1.0).astype(BF16)
-            v_scr[slot, 2 * j + 1] = jnp.where(low, 1.0, values[:, cut]).astype(BF16)
-
-    mask_of = {1: (0, 0), 2: (1, 1), 3: (2, 3), 4: (2, 3)}
+        for head in range(HEADS):
+            odd = head % 2
+            cut = slice(head // 2 * 128, (head // 2 + 1) * 128)
+            k_cut, v_cut = keys[:, cut], values[:, cut]
+            mine = low if odd == 0 else jnp.logical_not(low)
+            v_scr[tile, head] = jnp.where(mine, v_cut, 1.0).astype(BF16)
+            if tile < 3:
+                other = tag(odd, tile - 1) if tile else 0.0
+                k_scr[tile, head] = jnp.where(mine, k_cut, other).astype(BF16)
+            else:
+                for part in range(HALVES):
+                    part_rows = slice(part * half, (part + 1) * half)
+                    k_scr[tile, head, pl.ds(part * half, half), :] = jnp.where(
+                        mine, k_cut[part_rows], tag(odd, 2 + part)
+                    ).astype(BF16)
 
     def group(head, rows, tiles, start):
         query = q_scr[head, rows, :]
-        scores = [dot_t(query, k_scr[tile, head // 2]) for tile in tiles]
+        scores = [dot_t(query, k_scr[tile, head]) for tile in tiles]
         best = start
-        for tile, score in zip(tiles, scores):
-            sides = [score[:, :128], score[:, 128:]]
-            if tile and mask_of[tile][0] == mask_of[tile][1]:
-                top = jnp.maximum(*sides) - bias[mask_of[tile][0], rows, :]
-            elif tile:
-                top = jnp.maximum(*(x - bias[m, rows, :] for x, m in zip(sides, mask_of[tile])))
-            else:
-                top = jnp.maximum(*sides)
+        for score in scores:
+            top = jnp.maximum(score[:, :128], score[:, 128:])
             best = top if best is None else jnp.maximum(best, top)
         best = jnp.broadcast_to(jnp.max(best, axis=-1, keepdims=True), best.shape)
+        shift = jnp.concatenate([best, best], axis=1)
         result = None
         for tile, score in zip(tiles, scores):
-            if tile:
-                shift = jnp.concatenate([best + bias[m, rows, :] for m in mask_of[tile]], axis=1)
-            else:
-                shift = jnp.concatenate([best, best], axis=1)
-            weights = jnp.exp(score - shift).astype(BF16)
-            term = dot(weights, v_scr[tile, head])
+            term = dot(jnp.exp2(score - shift).astype(BF16), v_scr[tile, head])
             result = term if result is None else result + term
         return best, result
 
     def merged(head, rows, tiles):
         before = m_scr[head, rows, :]
         best, result = group(head, rows, tiles, before)
-        return best, r_scr[head, rows, :] * jnp.exp(before - best) + result
+        return best, r_scr[head, rows, :] * jnp.exp2(before - best) + result
 
     everything = pl.ds(0, mesh_rows)
 
@@ -358,11 +370,11 @@
     for layer in range(LAYERS):
         need(v_wq, v_wk, v_wv)
         value = xs[layer]
-        queries = dot(value, v_wq[layer]) * 0.125
+        queries = dot(value, v_wq[layer]) * (0.125 * LOG2E)
         for j in range(PAIRS):
             cut = queries[:, j * 128 : (j + 1) * 128]
-            q_scr[2 * j] = jnp.where(low, cut, 0.0).astype(BF16)
-            q_scr[2 * j + 1] = jnp.where(low, 0.0, cut).astype(BF16)
+            q_scr[2 * j] = jnp.where(low, cut, bias[0]).astype(BF16)
+            q_scr[2 * j + 1] = jnp.where(low, bias[1], cut).astype(BF16)
         project(layer, 0, value)
         arrived(layer, "partner", 0, 1)
         project(layer, 1, rx[layer, 0])
@@ -475,6 +487,7 @@
     phases = LAYERS + 1
     scratch = [pltpu.VMEM(operand.shape, operand.dtype) for operand in operands] + [
         pltpu.VMEM((grid_rows, width), BF16),
+        pltpu.VMEM((grid_rows, width), BF16),
         pltpu.VMEM((4, mesh_rows, width), BF16),
         pltpu.VMEM((4, 8, mesh_rows), F32),
         pltpu.VMEM((4, 8, mesh_rows), F32),
@@ -482,11 +495,11 @@
         pltpu.VMEM((mesh_rows, width), F32),
         pltpu.VMEM((mesh_rows, width), F32),
         pltpu.VMEM((mesh_rows, width), F32),
-        pltpu.VMEM((4, mesh_rows, 128), F32),
+        pltpu.VMEM((2, mesh_rows, 128), F32),
         pltpu.VMEM((phases, mesh_rows, width), BF16),
         pltpu.VMEM((phases, 4, mesh_rows, width), BF16),
         pltpu.VMEM((HEADS, mesh_rows, 128), BF16),
-        pltpu.VMEM((5, PAIRS, mesh_rows, 128), BF16),
+        pltpu.VMEM((5, HEADS, mesh_rows, 128), BF16),
         pltpu.VMEM((5, HEADS, mesh_rows, 128), BF16),
         pltpu.VMEM((HEADS, mesh_rows, 128), F32),
         pltpu.VMEM((HEADS, mesh_rows, 128), F32),
@@ -501,7 +514,7 @@
     ]
     return pl.pallas_call(
         functools.partial(kernel, count),
-        out_shape=jax.ShapeDtypeStruct((grid_rows, channels), BF16),
+        out_shape=pltpu.VMEM((grid_rows, channels), BF16),
         in_specs=[pl.BlockSpec(memory_space=pl.ANY)] * len(operands),
         out_specs=pl.BlockSpec(memory_space=pltpu.VMEM),
         scratch_shapes=scratch,

time: 69.1 us -> 67.2 us (0.973)
  local copies, waits for them, and re-layouts: 1.67 us -> 0.71 us
  Pallas kernels: 67.3 us -> 66.4 us
    unnamed x1, local copies, waits for them, and re-layouts: 1.67 us -> 0.71 us
    pallas_call x1, Pallas kernels: 67.3 us -> 66.4 us  [body(): pl.pallas_call(functools.partial(kernel, count), out_shape=pltpu.VMEM((gr...]
where the time goes in v3:
time: 67.2 us; the launch traced here: 67.1 us
  Pallas kernels  66.4 us (99%)
  local copies, waits for them, and re-layouts  0.71 us (1%)
    pallas_call x1, Pallas kernels, body(): pl.pallas_call(functools.partial(kernel, count), out_shape=pltpu.VMEM((gr...  66.4 us

profile of v3, /device:TPU:37, one launch (start us, length us, event | category | flops | bytes accessed | tf_op | source)
XLA Modules:
  0.0 67.1 jit_solution(12724986595622702505)
XLA Ops:
  0.0 66.4 %step.1 = bf16[1024,128]{1,0:T(8,128)(2,1)S(1)} custom-call(bf16[1024,128]{1,0:T(8,128)(2,1)} %grid_in.1, s32[1,1024]{1,0:T(1,128)} %bitcast.5, s32[1,1024]{1,0:T(1,128)} %bitcast.6, s32[4,256]{1,0:T(4,128)} %bitcast.7, bf16[256,512]{1,0:T(8,128)(2,1)} %mesh_embed.1, bf16[128,512]{1,0:T(8,128)(2,1)} %w_in.1, bf16[4,128]{1,0:T(4,128)(2,1)} %bitcast.8, ...), custom_call_target="tpu_custom_call" | custom-call | tf_op jit(solution)/shard_map/step/pallas_call | solution.py:515
  66.4 0.7 %copy.23 = bf16[1024,128]{1,0:T(8,128)(2,1)} copy(bf16[1024,128]{1,0:T(8,128)(2,1)S(1)} %step.1) | data formatting | bytes 524288

commit v4 on v3

--- a/solution.py
+++ b/solution.py
@@ -88,6 +88,8 @@
     v_wdec,
     v_whead,
     v_wfinal,
+    w_first,
+    w_last,
     hidden,
     feat,
     psend,
@@ -229,26 +231,6 @@
     sums, own_counts = partial(0)
     pown[...] = sums
 
-    need(v_wgrid)
-    for step in range(grid_rows // mesh_rows):
-        rows = pl.ds(step * mesh_rows, mesh_rows)
-        feat[rows, :] = dot(hidden[rows, :], v_wgrid[...]).astype(BF16)
-
-    code_columns = to_columns(code.astype(F32))
-    lane = lax.broadcasted_iota(jnp.int32, (1, mesh_rows), 1).astype(F32)
-    code_wide = jnp.concatenate([code_columns, code_columns], axis=1)
-    base = (side * mesh_rows).astype(F32)
-    left = lane < half
-    wanted = (
-        lane,
-        lane - base,
-        lane - 2 * base,
-        jnp.where(left, lane + 2 * base, lane - half + base),
-        jnp.where(left, lane + half + 2 * base, lane + base),
-    )
-    for tile, node in enumerate(wanted):
-        gather[tile] = jnp.where(code_wide == node, 1.0, 0.0).astype(BF16)
-
     need(v_mask)
     columns = [to_columns(v_mask[pl.ds(c, 1), :].astype(F32)) for c in range(4)]
     minus = jnp.zeros((mesh_rows, 128), F32) + core.astype(F32) > 0.5
@@ -269,6 +251,15 @@
         for kind, value in enumerate(by_slot):
             total = total + jnp.where(value > 0.5, 0.0, -BIG) * tag(odd, kind)
         bias[odd] = total
+
+    def product(target, left, right):
+        for step in range(width // mesh_rows):
+            rows = pl.ds(step * mesh_rows, mesh_rows)
+            target[rows, :] = dot(left[rows, :], right[...]).astype(BF16)
+
+    need(v_wgrid, v_wenc, v_wdec, v_whead)
+    product(w_first, v_wgrid, v_wenc)
+    product(w_last, v_wdec, v_whead)
 
     far_sends = {}
 
@@ -313,8 +304,7 @@
         summed = pown[rows, :] + erecv[1, rows, :].astype(F32)
         summed = summed + erecv[2, rows, :].astype(F32) + erecv[3, rows, :].astype(F32)
         mean_hidden = (summed * scale[h * half : (h + 1) * half]).astype(BF16)
-        mean_rows = dot(mean_hidden, v_wgrid[...]).astype(BF16)
-        value = v_embed[rows, :].astype(F32) + dot(mean_rows, v_wenc[...])
+        value = v_embed[rows, :].astype(F32) + dot(mean_hidden, w_first[...])
         state[rows, :] = value
         xs[0, rows, :] = rms(value, v_again[pl.ds(0, 1), :].astype(F32)).astype(BF16)
         broadcast(0, h)
@@ -339,9 +329,11 @@
                         mine, k_cut[part_rows], tag(odd, 2 + part)
                     ).astype(BF16)
 
-    def group(head, rows, tiles, start):
+    def score_all(head, rows, tiles):
         query = q_scr[head, rows, :]
-        scores = [dot_t(query, k_scr[tile, head]) for tile in tiles]
+        return [dot_t(query, k_scr[tile, head]) for tile in tiles]
+
+    def soften(head, tiles, scores, start):
         best = start
         for score in scores:
             top = jnp.maximum(score[:, :128], score[:, 128:])
@@ -354,18 +346,26 @@
             result = term if result is None else result + term
         return best, result
 
-    def merged(head, rows, tiles):
-        before = m_scr[head, rows, :]
-        best, result = group(head, rows, tiles, before)
-        return best, r_scr[head, rows, :] * jnp.exp2(before - best) + result
+    def attention(rows, tiles, fresh, consume):
+        coming = score_all(0, rows, tiles)
+        for head in range(HEADS):
+            scores = coming
+            if head + 1 < HEADS:
+                coming = score_all(head + 1, rows, tiles)
+            before = None if fresh else m_scr[head, rows, :]
+            best, result = soften(head, tiles, scores, before)
+            if not fresh:
+                result = r_scr[head, rows, :] * jnp.exp2(before - best) + result
+            consume(head, best, result)
 
     everything = pl.ds(0, mesh_rows)
 
+    def keep(head, best, result):
+        m_scr[head] = best
+        r_scr[head] = result
+
     def absorb(tile):
-        for head in range(HEADS):
-            best, result = merged(head, everything, (tile,))
-            m_scr[head] = best
-            r_scr[head] = result
+        attention(everything, (tile,), False, keep)
 
     for layer in range(LAYERS):
         need(v_wq, v_wk, v_wv)
@@ -378,13 +378,14 @@
         project(layer, 0, value)
         arrived(layer, "partner", 0, 1)
         project(layer, 1, rx[layer, 0])
-        for head in range(HEADS):
-            best, result = group(head, everything, (0, 1), None)
-            m_scr[head] = best
-            r_scr[head] = result
+
+        def keep_first(head, best, result):
+            keep(head, best, result)
             if head == 5:
                 forward(layer, 0)
                 rest(layer, 1)
+
+        attention(everything, (0, 1), True, keep_first)
         arrived(layer, "behind", 0)
         arrived(layer, "passed", 0)
         project(layer, 3, rx[layer, 2])
@@ -395,28 +396,44 @@
         arrived(layer, "behind", 1)
         arrived(layer, "passed", 1)
         project(layer, 4, rx[layer, 3])
-        need(v_wo, v_mgain, v_wu, v_wd, v_dgain, v_wdec)
-        for h in range(HALVES):
+        need(v_wo, v_mgain, v_wu, v_wd, v_dgain)
+
+        def stages(h, layer=layer):
             rows = hrows[h]
-            for j in range(PAIRS):
-                parts = [merged(2 * j + odd, rows, (4,))[1] for odd in range(2)]
-                top = jnp.where(low, parts[0], parts[1])
-                bottom = pltpu.roll(jnp.where(low, parts[1], parts[0]), 64, 1)
-                att[rows, pl.ds(j * 128, 128)] = (top / bottom).astype(BF16)
-            if h:
-                rest(layer + 1, 0)
             value = state[rows, :] + dot(att[rows, :], v_wo[layer])
             normed = rms(value, v_mgain[pl.ds(layer, 1), :].astype(F32)).astype(BF16)
+            yield
             up = silu(dot(normed, v_wu[layer])).astype(BF16)
+            yield
             value = value + dot(up, v_wd[layer])
             if layer + 1 < LAYERS:
                 state[rows, :] = value
                 sent = rms(value, v_again[pl.ds(layer + 1, 1), :].astype(F32)).astype(BF16)
             else:
                 decoded = rms(value, as_row(v_dgain)).astype(BF16)
-                sent = dot(decoded, v_wdec[...]).astype(BF16)
+                yield
+                sent = dot(decoded, w_last[...]).astype(BF16)
             xs[layer + 1, rows, :] = sent
             broadcast(layer + 1, h)
+
+        running = iter(())
+        for h in range(HALVES):
+            parts = {}
+
+            def finish(head, best, result, rows=hrows[h], parts=parts, running=running):
+                parts[head % 2] = result
+                if head % 2:
+                    top = jnp.where(low, parts[0], parts[1])
+                    bottom = pltpu.roll(jnp.where(low, parts[1], parts[0]), 64, 1)
+                    att[rows, pl.ds(head // 2 * 128, 128)] = (top / bottom).astype(BF16)
+                next(running, None)
+
+            attention(hrows[h], (4,), False, finish)
+            running = stages(h)
+            next(running, None)
+        rest(layer + 1, 0)
+        for _ in running:
+            pass
 
     steps = grid_rows // mesh_rows
     last = LAYERS
@@ -426,11 +443,29 @@
             rows = pl.ds(step * mesh_rows, mesh_rows)
             acc[rows, :] = acc[rows, :] + dot(gather[tile, rows, :], rx[last, slot])
 
+    code_columns = to_columns(code.astype(F32))
+    lane = lax.broadcasted_iota(jnp.int32, (1, mesh_rows), 1).astype(F32)
+    code_wide = jnp.concatenate([code_columns, code_columns], axis=1)
+    base = (side * mesh_rows).astype(F32)
+    left = lane < half
+    wanted = (
+        lane,
+        lane - base,
+        lane - 2 * base,
+        jnp.where(left, lane + 2 * base, lane - half + base),
+        jnp.where(left, lane + half + 2 * base, lane + base),
+    )
+    for tile, node in enumerate(wanted):
+        gather[tile] = jnp.where(code_wide == node, 1.0, 0.0).astype(BF16)
+
+    for step in range(steps):
+        rows = pl.ds(step * mesh_rows, mesh_rows)
+        feat[rows, :] = dot(hidden[rows, :], v_wgrid[...]).astype(BF16)
     arrived(last, "partner", 0, 1)
     for step in range(steps):
         rows = pl.ds(step * mesh_rows, mesh_rows)
         acc[rows, :] = (
-            feat[rows, :].astype(F32)
+            dot(feat[rows, :], v_whead[...])
             + dot(gather[0, rows, :], xs[last])
             + dot(gather[1, rows, :], rx[last, 0])
         )
@@ -442,13 +477,12 @@
     add(3, 2)
     forward(last, 1)
     add(2, 1)
-    need(v_whead, v_wfinal)
+    need(v_wfinal)
     arrived(last, "behind", 1)
     arrived(last, "passed", 1)
     for step in range(steps):
         rows = pl.ds(step * mesh_rows, mesh_rows)
-        mixed = (acc[rows, :] + dot(gather[4, rows, :], rx[last, 3])).astype(BF16)
-        head_rows = silu(dot(mixed, v_whead[...])).astype(BF16)
+        head_rows = silu(acc[rows, :] + dot(gather[4, rows, :], rx[last, 3])).astype(BF16)
         out[rows, :] = dot(head_rows, v_wfinal[...]).astype(BF16)
     for copy in started:
         copy.wait_send()
@@ -486,6 +520,8 @@
     ]
     phases = LAYERS + 1
     scratch = [pltpu.VMEM(operand.shape, operand.dtype) for operand in operands] + [
+        pltpu.VMEM((width, width), BF16),
+        pltpu.VMEM((width, width), BF16),
         pltpu.VMEM((grid_rows, width), BF16),
         pltpu.VMEM((grid_rows, width), BF16),
         pltpu.VMEM((4, mesh_rows, width), BF16),

time: 67.2 us -> 65.7 us (0.978)
  Pallas kernels: 66.4 us -> 64.9 us
    pallas_call x1, Pallas kernels: 66.4 us -> 64.9 us  [body(): pl.pallas_call(functools.partial(kernel, count), out_shape=pltpu.VMEM((gr...]
where the time goes in v4:
time: 65.7 us; the launch traced here: 65.6 us
  Pallas kernels  64.9 us (99%)
  local copies, waits for them, and re-layouts  0.71 us (1%)
    pallas_call x1, Pallas kernels, body(): pl.pallas_call(functools.partial(kernel, count), out_shape=pltpu.VMEM((gr...  64.9 us

profile of v4, /device:TPU:37, one launch (start us, length us, event | category | flops | bytes accessed | tf_op | source)
XLA Modules:
  0.0 65.6 jit_solution(13101445716608604665)
XLA Ops:
  0.0 64.9 %step.1 = bf16[1024,128]{1,0:T(8,128)(2,1)S(1)} custom-call(bf16[1024,128]{1,0:T(8,128)(2,1)} %grid_in.1, s32[1,1024]{1,0:T(1,128)} %bitcast.5, s32[1,1024]{1,0:T(1,128)} %bitcast.6, s32[4,256]{1,0:T(4,128)} %bitcast.7, bf16[256,512]{1,0:T(8,128)(2,1)} %mesh_embed.1, bf16[128,512]{1,0:T(8,128)(2,1)} %w_in.1, bf16[4,128]{1,0:T(4,128)(2,1)} %bitcast.8, ...), custom_call_target="tpu_custom_call" | custom-call | tf_op jit(solution)/shard_map/step/pallas_call | solution.py:551
  64.9 0.7 %copy.23 = bf16[1024,128]{1,0:T(8,128)(2,1)} copy(bf16[1024,128]{1,0:T(8,128)(2,1)S(1)} %step.1) | data formatting | bytes 524288

commit v5 on v4

--- a/solution.py
+++ b/solution.py
@@ -333,30 +333,37 @@
         query = q_scr[head, rows, :]
         return [dot_t(query, k_scr[tile, head]) for tile in tiles]
 
-    def soften(head, tiles, scores, start):
+    def soften(scores, start):
         best = start
         for score in scores:
             top = jnp.maximum(score[:, :128], score[:, 128:])
             best = top if best is None else jnp.maximum(best, top)
         best = jnp.broadcast_to(jnp.max(best, axis=-1, keepdims=True), best.shape)
         shift = jnp.concatenate([best, best], axis=1)
-        result = None
-        for tile, score in zip(tiles, scores):
-            term = dot(jnp.exp2(score - shift).astype(BF16), v_scr[tile, head])
-            result = term if result is None else result + term
-        return best, result
+        return best, [jnp.exp2(score - shift).astype(BF16) for score in scores]
 
     def attention(rows, tiles, fresh, consume):
+        def close(head, before, best, weights):
+            result = None
+            for tile, weight in zip(tiles, weights):
+                term = dot(weight, v_scr[tile, head])
+                result = term if result is None else result + term
+            if not fresh:
+                result = r_scr[head, rows, :] * jnp.exp2(before - best) + result
+            consume(head, best, result)
+
         coming = score_all(0, rows, tiles)
+        held = None
         for head in range(HEADS):
             scores = coming
             if head + 1 < HEADS:
                 coming = score_all(head + 1, rows, tiles)
             before = None if fresh else m_scr[head, rows, :]
-            best, result = soften(head, tiles, scores, before)
-            if not fresh:
-                result = r_scr[head, rows, :] * jnp.exp2(before - best) + result
-            consume(head, best, result)
+            best, weights = soften(scores, before)
+            if held is not None:
+                close(*held)
+            held = (head, before, best, weights)
+        close(*held)
 
     everything = pl.ds(0, mesh_rows)
 
@@ -364,8 +371,13 @@
         m_scr[head] = best
         r_scr[head] = result
 
-    def absorb(tile):
-        attention(everything, (tile,), False, keep)
+    def absorb(tile, after=None):
+        def keep_some(head, best, result):
+            keep(head, best, result)
+            if head == 3 and after is not None:
+                after()
+
+        attention(everything, (tile,), False, keep_some)
 
     for layer in range(LAYERS):
         need(v_wq, v_wk, v_wv)
@@ -389,8 +401,7 @@
         arrived(layer, "behind", 0)
         arrived(layer, "passed", 0)
         project(layer, 3, rx[layer, 2])
-        absorb(3)
-        forward(layer, 1)
+        absorb(3, functools.partial(forward, layer, 1))
         project(layer, 2, rx[layer, 1])
         absorb(2)
         arrived(layer, "behind", 1)

time: 65.7 us -> 65.9 us (level)
  no operation moved by 1% of the time
where the time goes in v5:
time: 65.9 us; the launch traced here: 65.7 us
  Pallas kernels  65 us (99%)
  local copies, waits for them, and re-layouts  0.71 us (1%)
    pallas_call x1, Pallas kernels, body(): pl.pallas_call(functools.partial(kernel, count), out_shape=pltpu.VMEM((gr...  65 us

profile of v5, /device:TPU:37, one launch (start us, length us, event | category | flops | bytes accessed | tf_op | source)
XLA Modules:
  0.0 65.7 jit_solution(2530003606153527449)
XLA Ops:
  0.0 65.0 %step.1 = bf16[1024,128]{1,0:T(8,128)(2,1)S(1)} custom-call(bf16[1024,128]{1,0:T(8,128)(2,1)} %grid_in.1, s32[1,1024]{1,0:T(1,128)} %bitcast.5, s32[1,1024]{1,0:T(1,128)} %bitcast.6, s32[4,256]{1,0:T(4,128)} %bitcast.7, bf16[256,512]{1,0:T(8,128)(2,1)} %mesh_embed.1, bf16[128,512]{1,0:T(8,128)(2,1)} %w_in.1, bf16[4,128]{1,0:T(4,128)(2,1)} %bitcast.8, ...), custom_call_target="tpu_custom_call" | custom-call | tf_op jit(solution)/shard_map/step/pallas_call | solution.py:562
  65.0 0.7 %copy.23 = bf16[1024,128]{1,0:T(8,128)(2,1)} copy(bf16[1024,128]{1,0:T(8,128)(2,1)S(1)} %step.1) | data formatting | bytes 524288
